TPU v7x, 8 devices: a whole 2x2x1 slice. The times are simulated.
8 devices in a mesh: dp: 2 (over z, y), sp: 4 (over x, core).
Axes of the slice: x: 2, y: 2, z: 1, core: 2. Of those that a mesh axis runs over, the one named last changes fastest.
Arguments:
- hidden: bfloat16 [32, 1024, 768], P('dp', 'sp'), parts along dimension 0
- pos_ids: int32 [32, 1024], P('dp', 'sp'), parts along dimension 0
- block_ids: int32 [32, 1024], P('dp', 'sp'), parts along dimension 0
- ctx_len: int32 [32], P('dp'), parts along dimension 0
- ln_gamma: bfloat16 [768], replicated
- ln_beta: bfloat16 [768], replicated
- w_qkv: bfloat16 [768, 12, 3, 64], replicated
- b_qkv: bfloat16 [12, 3, 64], replicated
- w_dense: bfloat16 [768, 768], replicated
- b_dense: bfloat16 [768], replicated
Outputs:
- output 1: bfloat16 [32, 1024, 768], P('dp', 'sp'), parts along dimension 0
- output 2: bfloat16 [32, 1024, 12, 64], P('dp', None, 'sp'), parts along dimension 0
- output 3: bfloat16 [32, 1024, 12, 64], P('dp', None, 'sp'), parts along dimension 0
There are 2 independent parts. A program takes and returns all parts, laid end to end along the dimension named above; an argument that names none is the same for every part.
All inputs are finite; a program needn't handle non-finite values.
Results may differ from a plain program's by a relative error of at most 0.00593733.
Values are sent between devices in bfloat16 or wider.
A program may use at most 1 GiB of HBM per device.

v0:
```python
import functools
import math
import numpy as np
import jax
import jax.numpy as jnp
from jax import lax
from jax.experimental import pallas as pl
from jax.experimental.pallas import tpu as pltpu
from jax.sharding import PartitionSpec as P

ALPHA = math.sqrt(56.0)
ROPE_BASE = 10000.0
LN_EPS = 1e-5
LOG2E = 1.4426950408889634
CHUNKS = (3, 4, 3, 3, 3)
F32 = jnp.float32
BF16 = jnp.bfloat16


def mm(a, b):
    return jnp.dot(a, b, preferred_element_type=F32)


def row_vector(ref):
    return ref[...].astype(F32).reshape(1, ref.shape[0])


def norm_kernel(plan, h_ref, g_ref, b_ref, *o_refs):
    def row(r):
        x = h_ref[r].astype(F32)
        x = x - jnp.mean(x, axis=-1, keepdims=True)
        var = jnp.mean(x * x, axis=-1, keepdims=True)
        y = x * lax.rsqrt(var + LN_EPS) * row_vector(g_ref) + row_vector(b_ref)
        return y.astype(BF16).T

    out = [row(r) for r in range(h_ref.shape[0])]
    step = pl.program_id(0)
    for (lo, hi, rows), o_ref in zip(plan, o_refs):
        @pl.when((step >= lo) & (step <= hi))
        def _():
            for i, r in enumerate(rows):
                o_ref[i] = out[r]


def rotate(x, cos_a, sin_a, cos_b, sin_b):
    u0, w0, u1, w1 = (x[16 * i:16 * i + 16] for i in range(4))
    parts = [u0 * cos_a - w0 * sin_a, w0 * cos_a + u0 * sin_a,
             u1 * cos_b - w1 * sin_b, w1 * cos_b + u1 * sin_b]
    return jnp.concatenate(parts, axis=0).astype(BF16)


def fold(accs, x, op):
    accs = list(accs) if accs else [None] * 4
    for i in range(x.shape[0] // 8):
        v = x[8 * i:8 * i + 8]
        accs[i % 4] = v if accs[i % 4] is None else op(accs[i % 4], v)
    return accs


def join(accs, op):
    return op(op(accs[0], accs[1]), op(accs[2], accs[3]))


def attn_kernel(heads, idx_ref, ctx_ref, row_ref, a0, a1, a2, a3, tab_ref, col_ref, w_ref, bias_ref, *rest):
    k_out, v_out, c_own, c_send, kn, kt, vt, qt, s_s, p_s, c_s, m_s = rest[-12:]
    hd = 64
    rows = heads * hd
    blk = a0.shape[2]
    ctx = ctx_ref[row_ref[0] + pl.program_id(0)]

    col = [jnp.concatenate([col_ref[0, 16 * i:16 * i + 16]] * 2, axis=1) for i in range(4)]
    for m, a_ref in enumerate((a0, a1, a2, a3)):
        j = idx_ref[m]
        a = a_ref[0]
        cos, sin = tab_ref[j, :16], tab_ref[j, 16:]
        inside = j * blk + lax.broadcasted_iota(jnp.int32, (1, blk), 1) < ctx
        tab = (jnp.where(inside, cos, col[0]), jnp.where(inside, sin, col[1]),
               jnp.where(inside, 1.0, cos * col[2] + sin * col[3]),
               jnp.where(inside, 0.0, sin * col[2] - cos * col[3]))

        def project(part):
            lo = part * rows
            b = bias_ref[lo:lo + rows]
            return (mm(w_ref[lo:lo + rows], a) + jnp.concatenate([b, b], axis=1)).astype(BF16)

        if m < 2:
            q = project(0)
            for h in range(heads):
                qh = rotate(q[h * hd:(h + 1) * hd].astype(F32), *tab)
                zero = jnp.zeros_like(qh)
                qt[m, h] = jnp.concatenate([qh, zero] if h % 2 == 0 else [zero, qh], axis=0)
        k = project(1)
        for p in range(heads // 2):
            pair = [rotate(k[(2 * p + i) * hd:(2 * p + i + 1) * hd].astype(F32), *tab) for i in range(2)]
            pair = jnp.concatenate(pair, axis=0)
            kt[j, p * 128:(p + 1) * 128] = pair
            kn[j, p] = pair.T
        vt[j] = project(2)

    half = rows // 2
    out_lo = pl.multiple_of(idx_ref[4] * half, half)

    def copy_out(j, carry):
        to = pl.ds(pl.multiple_of(j * blk, blk), blk)
        k_out[0, :, to] = kt[j, pl.ds(out_lo, half)]
        v_out[0, :, to] = vt[j, pl.ds(out_lo, half)]
        return carry

    lax.fori_loop(0, 4, copy_out, 0)

    scale = LOG2E / math.sqrt(hd)

    def attend(nb, masked, qi, jq):
        q_pos = jq * blk + lax.broadcasted_iota(jnp.int32, (1, blk), 1)
        limit = jnp.maximum(q_pos, ctx - 1)
        for kb in masked:
            key_pos = kb * blk + lax.broadcasted_iota(jnp.int32, (blk, blk), 0)
            m_s[kb % 2] = jnp.where(key_pos <= limit, 0.0, -jnp.inf)
        top, total, acc = {}, {}, {}
        for step in range(heads + 2):
            h0, h1, h2 = step, step - 1, step - 2
            if 0 <= h1 < heads:
                top[h1] = jnp.max(join(top[h1], jnp.maximum), axis=0, keepdims=True)
            for kb in range(nb):
                lo = kb * blk
                if h0 < heads:
                    s = mm(kn[kb, h0 // 2], qt[qi, h0])
                    if kb in masked:
                        s = s + m_s[kb % 2]
                    s_s[h0 % 2, lo:lo + blk] = s
                    top[h0] = fold(top.get(h0), s, jnp.maximum)
                if 0 <= h1 < heads:
                    for r in range(lo, lo + blk, 32):
                        e = jnp.exp2((s_s[h1 % 2, r:r + 32] - top[h1]) * scale)
                        total[h1] = fold(total.get(h1), e, jnp.add)
                        p_s[h1 % 2, r:r + 32] = e.astype(BF16)
                if 0 <= h2 < heads:
                    t = mm(vt[kb, h2 * hd:(h2 + 1) * hd], p_s[h2 % 2, lo:lo + blk])
                    acc[h2] = acc[h2] + t if kb else t
            if 0 <= h2 < heads:
                t = jnp.sum(join(total[h2], jnp.add), axis=0, keepdims=True)
                c_s[qi, h2 * hd:(h2 + 1) * hd] = (acc[h2] / t).astype(BF16)

    def query_block(qi, carry):
        jq = idx_ref[qi]
        pl.when(jq < 3)(functools.partial(attend, 3, (1, 2), qi, jq))
        pl.when(jq == 3)(functools.partial(attend, 4, (3,), qi, jq))
        return carry

    lax.fori_loop(0, 2, query_block, 0)
    c_own[0] = c_s[0].T
    c_send[0] = c_s[1].T


def dense_kernel(idx_ref, row_ref, own_ref, other_ref, a_ref, w0, w1, w2, w3, b_ref, *rest):
    o_ref = rest[-1]
    for r in range(o_ref.shape[0]):
        w = jnp.concatenate([w0[0], w1[0]], axis=0)
        acc = mm(own_ref[r], w)
        w = jnp.concatenate([w2[0], w3[0]], axis=0)
        acc = acc + mm(other_ref[r], w)
        o_ref[r] = (a_ref[r].T.astype(F32) * ALPHA + (acc + row_vector(b_ref))).astype(BF16)


def params(mib):
    return pltpu.CompilerParams(dimension_semantics=("arbitrary",), vmem_limit_bytes=mib * 1024 * 1024)


def solution(mesh):
    seq_spec = P('dp', 'sp', None)
    row_spec = P('dp', 'sp')
    head_spec = P('dp', None, 'sp', None)
    replicated = P()
    across_x = [(i, i ^ 2) for i in range(4)]
    across_core = [(i, i ^ 1) for i in range(4)]
    inv_freq = ROPE_BASE ** (-np.arange(0, 32, 2, dtype=np.float64) / 32)

    def local_block(hidden, pos_ids, block_ids, ctx_len, ln_gamma, ln_beta, w_qkv, b_qkv, w_dense, b_dense):
        n_rows, blk, width = hidden.shape
        n_heads, _, hd = b_qkv.shape
        heads = n_heads // 2
        rows = heads * hd
        half = rows // 2
        t = lax.axis_index('sp').astype(jnp.int32)
        core = t & 1
        idx = jnp.stack([t, t ^ 1, t ^ 2, t ^ 3, t >> 1, core, 2 + core, 1 - core, 3 - core])
        starts = np.concatenate([[0], np.cumsum(CHUNKS)]).tolist()

        def norm(chunks):
            first = starts[chunks[0]]
            step_rows = 2 if first % 2 == 0 and all(CHUNKS[i] % 2 == 0 for i in chunks) else 1
            plan, specs, shapes = [], [], []
            for i in chunks:
                r0, r1 = starts[i] - first, starts[i + 1] - first
                lo, hi = r0 // step_rows, (r1 - 1) // step_rows
                n = min(step_rows, r1 - r0)
                plan.append((lo, hi, [(r0 + k) % step_rows for k in range(n)]))
                specs.append(pl.BlockSpec((n, width, blk), lambda b, lo=lo, hi=hi: (jnp.clip(b - lo, 0, hi - lo), 0, 0)))
                shapes.append(jax.ShapeDtypeStruct((r1 - r0, width, blk), BF16))
            total = starts[chunks[-1] + 1] - first
            return list(pl.pallas_call(
                functools.partial(norm_kernel, plan),
                grid=(total // step_rows,),
                in_specs=[pl.BlockSpec((step_rows, blk, width), lambda b: (first // step_rows + b, 0, 0)),
                          pl.BlockSpec((width,), lambda b: (0,)),
                          pl.BlockSpec((width,), lambda b: (0,))],
                out_specs=specs,
                out_shape=shapes,
                compiler_params=params(60),
                cost_estimate=pl.CostEstimate(flops=total * 500_000_000, bytes_accessed=total * 800_000, transcendentals=0),
                name="norm",
            )(hidden, ln_gamma, ln_beta))

        a_own = norm([0])
        a_own += norm(list(range(1, len(CHUNKS))))
        a_x = []
        for a in a_own:
            a_x.append(lax.ppermute(a, 'sp', across_x))
        a_c = []
        for a in a_own:
            a_c.append(lax.ppermute(a, 'sp', across_core))

        last = pos_ids[:, blk - 1:].reshape(1, n_rows)
        last_x = lax.ppermute(last, 'sp', across_x)
        last_c = lax.ppermute(last, 'sp', across_core)
        last_xc = lax.ppermute(last_x, 'sp', across_core)
        mask_pos = jnp.where(t == 3, last, jnp.where(t == 2, last_c, jnp.where(t == 1, last_x, last_xc)))[0]
        freq = jnp.asarray(inv_freq.astype(np.float32))
        angle = jnp.stack([mask_pos, ctx_len - 1], axis=1).astype(F32)[:, :, None] * freq
        col = jnp.stack([jnp.cos(angle), jnp.sin(angle)], axis=2).reshape(n_rows, 64, 1)
        col = jnp.broadcast_to(col, (n_rows, 64, 128))
        fine = inv_freq[:, None] * np.arange(blk)
        fine_c, fine_s = np.cos(fine).astype(np.float32)[None], np.sin(fine).astype(np.float32)[None]
        coarse = inv_freq[None, :, None] * (np.arange(4) * blk)[:, None, None]
        coarse_c, coarse_s = np.cos(coarse).astype(np.float32), np.sin(coarse).astype(np.float32)
        tab = jnp.concatenate([fine_c * jnp.asarray(coarse_c) - fine_s * jnp.asarray(coarse_s),
                               fine_s * jnp.asarray(coarse_c) + fine_c * jnp.asarray(coarse_s)], axis=1)

        bias = b_qkv.transpose(1, 0, 2).reshape(3, 2, 2, half)
        bias = lax.dynamic_index_in_dim(bias, core, 2, keepdims=False).reshape(3 * rows, 1)
        bias = jnp.broadcast_to(bias.astype(F32), (3 * rows, 128))
        w, bias, col, tab = lax.optimization_barrier((w_qkv, bias, col, tab))
        w = w.transpose(2, 1, 3, 0).reshape(3, 2, 2, half, width)
        w = lax.dynamic_index_in_dim(w, core, 2, keepdims=False).reshape(3 * rows, width)
        wd = w_dense.reshape(4, half, width)

        row_of = [jnp.full((1,), r, jnp.int32) for r in starts[:-1]]

        keys = values = out = None

        def finish(item, out):
            i, own, other = item
            n = CHUNKS[i]
            extra = [] if out is None else [out]
            return pl.pallas_call(
                dense_kernel,
                grid_spec=pltpu.PrefetchScalarGridSpec(
                    num_scalar_prefetch=2,
                    grid=(n,),
                    in_specs=[pl.BlockSpec((1, blk, rows), lambda b, s, r: (b, 0, 0)),
                              pl.BlockSpec((1, blk, rows), lambda b, s, r: (b, 0, 0)),
                              pl.BlockSpec((1, width, blk), lambda b, s, r: (b, 0, 0))]
                    + [pl.BlockSpec((1, half, width), lambda b, s, r, k=k: (s[k], 0, 0)) for k in (5, 6, 7, 8)]
                    + [pl.BlockSpec((width,), lambda b, s, r: (0,))]
                    + [pl.BlockSpec(memory_space=pl.ANY)] * len(extra),
                    out_specs=pl.BlockSpec((1, blk, width), lambda b, s, r: (r[0] + b, 0, 0)),
                ),
                out_shape=jax.ShapeDtypeStruct((n_rows, blk, width), BF16),
                input_output_aliases={10: 0} if extra else {},
                compiler_params=params(24),
                cost_estimate=pl.CostEstimate(flops=n * 1_000_000_000, bytes_accessed=n * 2_000_000, transcendentals=0),
                name="dense",
            )(idx, row_of[i], own, other, a_own[i], wd, wd, wd, wd, b_dense, *extra)

        a_xc = {}

        def fetch(i, after):
            got = lax.optimization_barrier((a_x[i], *after))
            a_xc[i] = lax.ppermute(got[0], 'sp', across_core)

        fetch(0, (a_own[1], w, bias, col))
        pending = []
        for i, n in enumerate(CHUNKS):
            extra = [] if keys is None else [keys, values]
            a_spec = pl.BlockSpec((1, width, blk), lambda b, *_: (b, 0, 0))
            kv_shape = jax.ShapeDtypeStruct((n_rows, half, 4 * blk), BF16)
            kv_spec = pl.BlockSpec((1, half, 4 * blk), lambda b, i, c, r: (r[0] + b, 0, 0))
            c_shape = jax.ShapeDtypeStruct((n, blk, rows), BF16)
            c_spec = pl.BlockSpec((1, blk, rows), lambda b, *_: (b, 0, 0))
            attn = pl.pallas_call(
                functools.partial(attn_kernel, heads),
                grid_spec=pltpu.PrefetchScalarGridSpec(
                    num_scalar_prefetch=3,
                    grid=(n,),
                    in_specs=[a_spec] * 4 + [
                        pl.BlockSpec((4, 32, blk), lambda b, *_: (0, 0, 0)),
                        pl.BlockSpec((1, 64, 128), lambda b, i, c, r: (r[0] + b, 0, 0)),
                        pl.BlockSpec((3 * rows, width), lambda b, *_: (0, 0)),
                        pl.BlockSpec((3 * rows, 128), lambda b, *_: (0, 0))]
                    + [pl.BlockSpec(memory_space=pl.ANY)] * len(extra),
                    out_specs=[kv_spec, kv_spec, c_spec, c_spec],
                    scratch_shapes=[
                        pltpu.VMEM((4, heads // 2, blk, 128), BF16),
                        pltpu.VMEM((4, rows, blk), BF16),
                        pltpu.VMEM((4, rows, blk), BF16),
                        pltpu.VMEM((2, heads, 128, blk), BF16),
                        pltpu.VMEM((2, 4 * blk, blk), F32),
                        pltpu.VMEM((2, 4 * blk, blk), BF16),
                        pltpu.VMEM((2, rows, blk), BF16),
                        pltpu.VMEM((2, blk, blk), F32),
                    ],
                ),
                out_shape=[kv_shape, kv_shape, c_shape, c_shape],
                input_output_aliases={11: 0, 12: 1} if extra else {},
                compiler_params=params(28),
                cost_estimate=pl.CostEstimate(flops=n * 6_000_000_000, bytes_accessed=n * 4_000_000, transcendentals=0),
                name="attn",
            )
            keys, values, own, send = attn(idx, ctx_len, row_of[i], a_own[i], a_c[i], a_x[i], a_xc[i], tab, col, w, bias, *extra)
            other = lax.ppermute(send, 'sp', across_core)
            if i + 1 < len(CHUNKS):
                fetch(i + 1, (own,) + (() if out is None else (out,)))
            for item in pending:
                out = finish(item, out)
            pending = [(i, own, other)]
        for item in pending:
            out = finish(item, out)

        def by_heads(x):
            return x.reshape(n_rows, n_heads // 4, hd, 4 * blk).transpose(0, 3, 1, 2)

        return out, by_heads(keys), by_heads(values)

    return jax.shard_map(local_block, mesh=mesh, in_specs=(seq_spec, row_spec, row_spec, P('dp'), replicated, replicated, replicated, replicated, replicated, replicated), out_specs=(seq_spec, head_spec, head_spec), check_vma=False)
```

profile of v0, /device:TPU:0, one launch (start us, length us, event | category | flops | bytes accessed | tf_op | source)
XLA Modules:
  0.0 192.1 jit_solution(11570243277918835820)
XLA Ops:
  0.6 0.9 slice_reduce_fusion
  1.5 3.3 %collective-permute-start.11 = (s32[1,16]{1,0:T(1,128)S(1)}, s32[1,16]{1,0:T(1,128)S(1)}, u32[]{:S(2)}, u32[]{:S(2)}) collective-permute-start(s32[1,16]{1,0:T(1,128)S(1)} %bitcast.54), channel_id=1, source_target_pairs={{0,2},{1,3},{2,0},{3,1},{4,6},{5,7},{6,4},{7,5}} | collective-permute-start | bytes 200 | tf_op jit(solution)/shard_map/ppermute | solution.py:224
  4.8 3.7 %norm.3.a0.a_ref = bf16[3,768,256]{2,1,0:T(8,128)(2,1)} custom-call(bf16[16,256,768]{2,1,0:T(8,128)(2,1)} %h_ref.3, bf16[768]{0:T(1024)(128)(2,1)} %g_ref.3, bf16[768]{0:T(1024)(128)(2,1)} %b_ref.8), custom_call_target="tpu_custom_call" | custom-call | flops 1500000000 | bytes 2400000 | tf_op jit(solution)/shard_map/norm/pallas_call | solution.py:201
  9.2 12.1 %norm.2 = (bf16[4,768,256]{2,1,0:T(8,128)(2,1)}, bf16[3,768,256]{2,1,0:T(8,128)(2,1)}, bf16[3,768,256]{2,1,0:T(8,128)(2,1)}, bf16[3,768,256]{2,1,0:T(8,128)(2,1)}) custom-call(bf16[16,256,768]{2,1,0:T(8,128)(2,1)} %h_ref.3, bf16[768]{0:T(1024)(128)(2,1)} %g_ref.3, bf16[768]{0:T(1024)(128)(2,1)} %b_ref.8), custom_call_target="tpu_custom_call" | custom-call | flops 6499999744 | bytes 10400000 | tf_op jit(solution)/shard_map/norm/pallas_call | solution.py:201
  21.6 0.7 pad_maximum_fusion.tab_ref
  22.5 1.1 collective-permute-done.12
  23.9 1.0 broadcast_in_dim.16.col_ref
  25.1 2.2 %copy.37 = bf16[768,12,3,64]{0,3,1,2:T(8,128)(2,1)S(1)} copy(bf16[768,12,3,64]{0,3,2,1:T(8,128)(2,1)} %param.20) | data formatting | bytes 7077888 | tf_op jit(solution)/shard_map/optimization_barrier | solution.py:242
  27.5 9.9 %collective-permute-done.9.a2 = bf16[3,768,256]{2,1,0:T(8,128)(2,1)} collective-permute-done((bf16[3,768,256]{2,1,0:T(8,128)(2,1)}, bf16[3,768,256]{2,1,0:T(8,128)(2,1)}, u32[]{:S(2)}, u32[]{:S(2)}) %collective-permute-start.9) | collective-permute-done | bytes 1179680 | tf_op jit(solution)/shard_map/ppermute | solution.py:218
  38.0 2.6 %collective-permute-done.13.a3 = bf16[3,768,256]{2,1,0:T(8,128)(2,1)} collective-permute-done((bf16[3,768,256]{2,1,0:T(8,128)(2,1)}, bf16[3,768,256]{2,1,0:T(8,128)(2,1)}, u32[]{:S(2)}, u32[]{:S(2)}) %collective-permute-start.13) | collective-permute-done | bytes 1179680 | tf_op jit(solution)/shard_map/ppermute | solution.py:279
  40.6 1.0 copy-done.5
  41.6 0.9 copy-done.7
  42.5 19.7 %attn.5 = (bf16[16,192,1024]{2,1,0:T(8,128)(2,1)}, bf16[16,192,1024]{2,1,0:T(8,128)(2,1)}, bf16[3,256,384]{2,1,0:T(8,128)(2,1)S(1)}, bf16[3,256,384]{2,1,0:T(8,128)(2,1)S(1)}) custom-call(s32[9]{0:T(128)S(1)} %stack.52.idx_ref, s32[16]{0:T(128)S(1)} %copy-done.10, s32[1]{0:T(128)} %constant.15.clone.1.row_ref, bf16[3,768,256]{2,1,0:T(8,128)(2,1)S(1)} %copy-done.1, ...), custom_call_target="tpu_custom_call" | custom-call | flops 17999998976 | bytes 12000000 | tf_op jit(solution)/shard_map/attn/pallas_call | solution.py:319
  62.2 12.3 %collective-permute-done.7.a2 = bf16[4,768,256]{2,1,0:T(8,128)(2,1)} collective-permute-done((bf16[4,768,256]{2,1,0:T(8,128)(2,1)}, bf16[4,768,256]{2,1,0:T(8,128)(2,1)}, u32[]{:S(2)}, u32[]{:S(2)}) %collective-permute-start.7) | collective-permute-done | bytes 1572896 | tf_op jit(solution)/shard_map/ppermute | solution.py:218
  75.0 3.1 %collective-permute-done.14.a3 = bf16[4,768,256]{2,1,0:T(8,128)(2,1)S(1)} collective-permute-done((bf16[4,768,256]{2,1,0:T(8,128)(2,1)}, bf16[4,768,256]{2,1,0:T(8,128)(2,1)S(1)}, u32[]{:S(2)}, u32[]{:S(2)}) %collective-permute-start.14) | collective-permute-done | bytes 1572896 | tf_op jit(solution)/shard_map/ppermute | solution.py:279
  78.1 25.6 %attn.6 = (bf16[16,192,1024]{2,1,0:T(8,128)(2,1)}, bf16[16,192,1024]{2,1,0:T(8,128)(2,1)}, bf16[4,256,384]{2,1,0:T(8,128)(2,1)S(1)}, bf16[4,256,384]{2,1,0:T(8,128)(2,1)S(1)}) custom-call(s32[9]{0:T(128)S(1)} %stack.52.idx_ref, s32[16]{0:T(128)S(1)} %copy-done.10, s32[1]{0:T(128)} %constant.14.clone.1.row_ref, ...), custom_call_target="tpu_custom_call", output_to_operand_aliasing={{0}: (11, {}), {1}: (12, {})} | custom-call | flops 24000000000 | bytes 16000000 | tf_op jit(solution)/shard_map/attn/pallas_call | solution.py:319
  104.3 2.0 %collective-permute-start.3 = (bf16[3,768,256]{2,1,0:T(8,128)(2,1)S(1)}, bf16[3,768,256]{2,1,0:T(8,128)(2,1)S(1)}, u32[]{:S(2)}, u32[]{:S(2)}) collective-permute-start(bf16[3,768,256]{2,1,0:T(8,128)(2,1)S(1)} %copy-done.3), channel_id=1, source_target_pairs={{0,2},{1,3},{2,0},{3,1},{4,6},{5,7},{6,4},{7,5}} | collective-permute-start | bytes 3538952 | tf_op jit(solution)/shard_map/ppermute | solution.py:218
  106.3 1.1 collective-permute-done.16.other_ref
  107.5 3.2 %dense.5.rest_0_ = bf16[16,256,768]{2,1,0:T(8,128)(2,1)} custom-call(s32[9]{0:T(128)S(1)} %stack.52.idx_ref, s32[1]{0:T(128)} %constant.15.clone.1.row_ref, bf16[3,256,384]{2,1,0:T(8,128)(2,1)S(1)} %get-tuple-element.45.own_ref, bf16[3,256,384]{2,1,0:T(8,128)(2,1)S(1)} %collective-permute-done.16.other_ref, bf16[3,768,256]{2,1,0:T(8,128)(2,1)S(1)} %copy-done.1, ...), custom_call_target="tpu_custom_call" | custom-call | flops 3000000000 | bytes 6000000 | tf_op jit(solution)/shard_map/dense/pallas_call | solution.py:255
  110.7 18.5 %attn.7 = (bf16[16,192,1024]{2,1,0:T(8,128)(2,1)}, bf16[16,192,1024]{2,1,0:T(8,128)(2,1)}, bf16[3,256,384]{2,1,0:T(8,128)(2,1)S(1)}, bf16[3,256,384]{2,1,0:T(8,128)(2,1)S(1)}) custom-call(s32[9]{0:T(128)S(1)} %stack.52.idx_ref, s32[16]{0:T(128)S(1)} %copy-done.10, s32[1]{0:T(128)} %constant.13.clone.1.row_ref, ...), custom_call_target="tpu_custom_call", output_to_operand_aliasing={{0}: (11, {}), {1}: (12, {})} | custom-call | flops 17999998976 | bytes 12000000 | tf_op jit(solution)/shard_map/attn/pallas_call | solution.py:319
  129.2 3.4 %collective-permute-done.3.a2 = bf16[3,768,256]{2,1,0:T(8,128)(2,1)S(1)} collective-permute-done((bf16[3,768,256]{2,1,0:T(8,128)(2,1)S(1)}, bf16[3,768,256]{2,1,0:T(8,128)(2,1)S(1)}, u32[]{:S(2)}, u32[]{:S(2)}) %collective-permute-start.3) | collective-permute-done | bytes 1179680 | tf_op jit(solution)/shard_map/ppermute | solution.py:218
  132.6 0.5 collective-permute-start.18
  133.1 1.7 collective-permute-start.1
  134.8 1.7 collective-permute-done.18.other_ref
  136.5 5.2 %dense.6.rest_0_ = bf16[16,256,768]{2,1,0:T(8,128)(2,1)} custom-call(s32[9]{0:T(128)S(1)} %stack.52.idx_ref, s32[1]{0:T(128)} %constant.14.clone.1.row_ref, bf16[4,256,384]{2,1,0:T(8,128)(2,1)S(1)} %get-tuple-element.49.own_ref, bf16[4,256,384]{2,1,0:T(8,128)(2,1)S(1)} %collective-permute-done.18.other_ref, ...), custom_call_target="tpu_custom_call", output_to_operand_aliasing={{}: (10, {})} | custom-call | flops 4000000000 | bytes 8000000 | tf_op jit(solution)/shard_map/dense/pallas_call | solution.py:255
  141.8 18.8 %attn.8 = (bf16[16,192,1024]{2,1,0:T(8,128)(2,1)}, bf16[16,192,1024]{2,1,0:T(8,128)(2,1)}, bf16[3,256,384]{2,1,0:T(8,128)(2,1)S(1)}, bf16[3,256,384]{2,1,0:T(8,128)(2,1)S(1)}) custom-call(s32[9]{0:T(128)S(1)} %stack.52.idx_ref, s32[16]{0:T(128)S(1)} %copy-done.10, s32[1]{0:T(128)} %constant.21.clone.1.row_ref, ...), custom_call_target="tpu_custom_call", output_to_operand_aliasing={{0}: (11, {}), {1}: (12, {})} | custom-call | flops 17999998976 | bytes 12000000 | tf_op jit(solution)/shard_map/attn/pallas_call | solution.py:319
  161.0 0.5 collective-permute-start.22
  161.5 2.3 %collective-permute-done.19.a3 = bf16[3,768,256]{2,1,0:T(8,128)(2,1)S(1)} collective-permute-done((bf16[3,768,256]{2,1,0:T(8,128)(2,1)S(1)}, bf16[3,768,256]{2,1,0:T(8,128)(2,1)S(1)}, u32[]{:S(2)}, u32[]{:S(2)}) %collective-permute-start.19) | collective-permute-done | bytes 1179680 | tf_op jit(solution)/shard_map/ppermute | solution.py:279
  163.8 18.5 %attn.9 = (bf16[16,192,1024]{2,1,0:T(8,128)(2,1)}, bf16[16,192,1024]{2,1,0:T(8,128)(2,1)}, bf16[3,256,384]{2,1,0:T(8,128)(2,1)S(1)}, bf16[3,256,384]{2,1,0:T(8,128)(2,1)S(1)}) custom-call(s32[9]{0:T(128)S(1)} %stack.52.idx_ref, s32[16]{0:T(128)S(1)} %copy-done.10, s32[1]{0:T(128)} %constant.20.clone.1.row_ref, ...), custom_call_target="tpu_custom_call", output_to_operand_aliasing={{0}: (11, {}), {1}: (12, {})} | custom-call | flops 17999998976 | bytes 12000000 | tf_op jit(solution)/shard_map/attn/pallas_call | solution.py:319
  182.5 3.2 %dense.7.rest_0_ = bf16[16,256,768]{2,1,0:T(8,128)(2,1)} custom-call(s32[9]{0:T(128)S(1)} %stack.52.idx_ref, s32[1]{0:T(128)} %constant.13.clone.1.row_ref, bf16[3,256,384]{2,1,0:T(8,128)(2,1)S(1)} %get-tuple-element.53.own_ref, bf16[3,256,384]{2,1,0:T(8,128)(2,1)S(1)} %collective-permute-done.22.other_ref, ...), custom_call_target="tpu_custom_call", output_to_operand_aliasing={{}: (10, {})} | custom-call | flops 3000000000 | bytes 6000000 | tf_op jit(solution)/shard_map/dense/pallas_call | solution.py:255
  185.7 3.2 %dense.8.rest_0_ = bf16[16,256,768]{2,1,0:T(8,128)(2,1)} custom-call(s32[9]{0:T(128)S(1)} %stack.52.idx_ref, s32[1]{0:T(128)} %constant.21.clone.1.row_ref, bf16[3,256,384]{2,1,0:T(8,128)(2,1)S(1)} %get-tuple-element.58.own_ref, bf16[3,256,384]{2,1,0:T(8,128)(2,1)S(1)} %collective-permute-done.21.other_ref, ...), custom_call_target="tpu_custom_call", output_to_operand_aliasing={{}: (10, {})} | custom-call | flops 3000000000 | bytes 6000000 | tf_op jit(solution)/shard_map/dense/pallas_call | solution.py:255
  188.9 3.2 %dense.9 = bf16[16,256,768]{2,1,0:T(8,128)(2,1)} custom-call(s32[9]{0:T(128)S(1)} %stack.52.idx_ref, s32[1]{0:T(128)} %constant.20.clone.1.row_ref, bf16[3,256,384]{2,1,0:T(8,128)(2,1)S(1)} %get-tuple-element.63.own_ref, bf16[3,256,384]{2,1,0:T(8,128)(2,1)S(1)} %collective-permute-done.20.other_ref, ...), custom_call_target="tpu_custom_call", output_to_operand_aliasing={{}: (10, {})} | custom-call | flops 3000000000 | bytes 6000000 | tf_op jit(solution)/shard_map/dense/pallas_call | solution.py:255
  (79 shorter events, 3.9 us)
Async XLA Ops:
  1.5 20.9 %collective-permute-start.11 = (s32[1,16]{1,0:T(1,128)S(1)}, s32[1,16]{1,0:T(1,128)S(1)}, u32[]{:S(2)}, u32[]{:S(2)}) collective-permute-start(s32[1,16]{1,0:T(1,128)S(1)} %bitcast.54), channel_id=1, source_target_pairs={{0,2},{1,3},{2,0},{3,1},{4,6},{5,7},{6,4},{7,5}} | collective-permute-start | bytes 200 | tf_op jit(solution)/shard_map/ppermute | solution.py:224
  4.8 17.6 %collective-permute-start.10 = (s32[1,16]{1,0:T(1,128)S(1)}, s32[1,16]{1,0:T(1,128)S(1)}, u32[]{:S(2)}, u32[]{:S(2)}) collective-permute-start(s32[1,16]{1,0:T(1,128)S(1)} %bitcast.55), channel_id=1, source_target_pairs={{0,1},{1,0},{2,3},{3,2},{4,5},{5,4},{6,7},{7,6}} | collective-permute-start | bytes 200 | tf_op jit(solution)/shard_map/ppermute | solution.py:225
  8.6 13.7 %copy-start.10 = (s32[16]{0:T(128)S(1)}, s32[16]{0:T(128)}, u32[]{:S(2)}) copy-start(s32[16]{0:T(128)} %ctx_ref.9) | copy-start | bytes 196
  8.6 14.9 %copy-start.16 = (f32[16]{0:T(128)S(1)}, f32[16]{0:T(128)}, u32[]{:S(2)}) copy-start(f32[16]{0:T(128)} %constant.42.clone) | copy-start | bytes 196
  8.6 28.7 %collective-permute-start.9 = (bf16[3,768,256]{2,1,0:T(8,128)(2,1)}, bf16[3,768,256]{2,1,0:T(8,128)(2,1)}, u32[]{:S(2)}, u32[]{:S(2)}) collective-permute-start(bf16[3,768,256]{2,1,0:T(8,128)(2,1)} %norm.3.a0.a_ref), channel_id=1, source_target_pairs={{0,2},{1,3},{2,0},{3,1},{4,6},{5,7},{6,4},{7,5}} | collective-permute-start | bytes 3538952 | tf_op jit(solution)/shard_map/ppermute | solution.py:218
  8.7 29.2 %collective-permute-start.8 = (bf16[3,768,256]{2,1,0:T(8,128)(2,1)}, bf16[3,768,256]{2,1,0:T(8,128)(2,1)}, u32[]{:S(2)}, u32[]{:S(2)}) collective-permute-start(bf16[3,768,256]{2,1,0:T(8,128)(2,1)} %norm.3.a0.a_ref), channel_id=1, source_target_pairs={{0,1},{1,0},{2,3},{3,2},{4,5},{5,4},{6,7},{7,6}} | collective-permute-start | bytes 3538952 | tf_op jit(solution)/shard_map/ppermute | solution.py:221
  22.4 1.2 collective-permute-start.12
  37.4 3.2 %collective-permute-start.13 = (bf16[3,768,256]{2,1,0:T(8,128)(2,1)}, bf16[3,768,256]{2,1,0:T(8,128)(2,1)}, u32[]{:S(2)}, u32[]{:S(2)}) collective-permute-start(bf16[3,768,256]{2,1,0:T(8,128)(2,1)} %collective-permute-done.9.a2), channel_id=1, source_target_pairs={{0,1},{1,0},{2,3},{3,2},{4,5},{5,4},{6,7},{7,6}} | collective-permute-start | bytes 3538952 | tf_op jit(solution)/shard_map/ppermute | solution.py:279
  37.4 37.1 %collective-permute-start.7 = (bf16[4,768,256]{2,1,0:T(8,128)(2,1)}, bf16[4,768,256]{2,1,0:T(8,128)(2,1)}, u32[]{:S(2)}, u32[]{:S(2)}) collective-permute-start(bf16[4,768,256]{2,1,0:T(8,128)(2,1)} %get-tuple-element.39.a0.a_ref), channel_id=1, source_target_pairs={{0,2},{1,3},{2,0},{3,1},{4,6},{5,7},{6,4},{7,5}} | collective-permute-start | bytes 4718600 | tf_op jit(solution)/shard_map/ppermute | solution.py:218
  37.6 37.4 %collective-permute-start.6 = (bf16[4,768,256]{2,1,0:T(8,128)(2,1)}, bf16[4,768,256]{2,1,0:T(8,128)(2,1)}, u32[]{:S(2)}, u32[]{:S(2)}) collective-permute-start(bf16[4,768,256]{2,1,0:T(8,128)(2,1)} %get-tuple-element.39.a0.a_ref), channel_id=1, source_target_pairs={{0,1},{1,0},{2,3},{3,2},{4,5},{5,4},{6,7},{7,6}} | collective-permute-start | bytes 4718600 | tf_op jit(solution)/shard_map/ppermute | solution.py:221
  38.0 36.5 %copy-start.4 = (bf16[3,768,256]{2,1,0:T(8,128)(2,1)S(1)}, bf16[3,768,256]{2,1,0:T(8,128)(2,1)}, u32[]{:S(2)}) copy-start(bf16[3,768,256]{2,1,0:T(8,128)(2,1)} %get-tuple-element.38.a0.a_ref) | copy-start | bytes 3538948
  42.5 35.6 %copy-start.6 = (f32[16,64,128]{2,1,0:T(8,128)S(1)}, f32[16,64,128]{2,1,0:T(8,128)}, u32[]{:S(2)}) copy-start(f32[16,64,128]{2,1,0:T(8,128)} %broadcast_in_dim.16.col_ref) | copy-start | bytes 1572868
  42.5 35.6 %copy-start.8 = (f32[4,32,256]{2,1,0:T(8,128)S(1)}, f32[4,32,256]{2,1,0:T(8,128)}, u32[]{:S(2)}) copy-start(f32[4,32,256]{2,1,0:T(8,128)} %pad_maximum_fusion.tab_ref) | copy-start | bytes 393220
  74.5 3.6 %collective-permute-start.14 = (bf16[4,768,256]{2,1,0:T(8,128)(2,1)}, bf16[4,768,256]{2,1,0:T(8,128)(2,1)S(1)}, u32[]{:S(2)}, u32[]{:S(2)}) collective-permute-start(bf16[4,768,256]{2,1,0:T(8,128)(2,1)} %collective-permute-done.7.a2), channel_id=1, source_target_pairs={{0,1},{1,0},{2,3},{3,2},{4,5},{5,4},{6,7},{7,6}} | collective-permute-start | bytes 4718600 | tf_op jit(solution)/shard_map/ppermute | solution.py:279
  74.5 29.3 %collective-permute-start.5 = (bf16[3,768,256]{2,1,0:T(8,128)(2,1)S(1)}, bf16[3,768,256]{2,1,0:T(8,128)(2,1)S(1)}, u32[]{:S(2)}, u32[]{:S(2)}) collective-permute-start(bf16[3,768,256]{2,1,0:T(8,128)(2,1)S(1)} %copy-done.4), channel_id=1, source_target_pairs={{0,2},{1,3},{2,0},{3,1},{4,6},{5,7},{6,4},{7,5}} | collective-permute-start | bytes 3538952 | tf_op jit(solution)/shard_map/ppermute | solution.py:218
  74.8 35.9 %collective-permute-start.4 = (bf16[3,768,256]{2,1,0:T(8,128)(2,1)S(1)}, bf16[3,768,256]{2,1,0:T(8,128)(2,1)S(1)}, u32[]{:S(2)}, u32[]{:S(2)}) collective-permute-start(bf16[3,768,256]{2,1,0:T(8,128)(2,1)S(1)} %copy-done.4), channel_id=1, source_target_pairs={{0,1},{1,0},{2,3},{3,2},{4,5},{5,4},{6,7},{7,6}} | collective-permute-start | bytes 3538952 | tf_op jit(solution)/shard_map/ppermute | solution.py:221
  78.1 26.2 %copy-start.3 = (bf16[3,768,256]{2,1,0:T(8,128)(2,1)S(1)}, bf16[3,768,256]{2,1,0:T(8,128)(2,1)}, u32[]{:S(2)}) copy-start(bf16[3,768,256]{2,1,0:T(8,128)(2,1)} %get-tuple-element.37.a0.a_ref) | copy-start | bytes 3538948
  78.1 29.3 %copy-start = (bf16[768,768]{1,0:T(8,128)(2,1)S(1)}, bf16[768,768]{1,0:T(8,128)(2,1)}, u32[]{:S(2)}) copy-start(bf16[768,768]{1,0:T(8,128)(2,1)} %param.22) | copy-start | bytes 3538948
  78.1 29.3 %copy-start.9 = (bf16[768]{0:T(1024)(128)(2,1)S(1)}, bf16[768]{0:T(1024)(128)(2,1)}, u32[]{:S(2)}) copy-start(bf16[768]{0:T(1024)(128)(2,1)} %b_ref.13) | copy-start | bytes 4612
  103.8 6.9 %collective-permute-start.15 = (bf16[3,768,256]{2,1,0:T(8,128)(2,1)S(1)}, bf16[3,768,256]{2,1,0:T(8,128)(2,1)S(1)}, u32[]{:S(2)}, u32[]{:S(2)}) collective-permute-start(bf16[3,768,256]{2,1,0:T(8,128)(2,1)S(1)} %collective-permute-done.5.a2), channel_id=1, source_target_pairs={{0,1},{1,0},{2,3},{3,2},{4,5},{5,4},{6,7},{7,6}} | collective-permute-start | bytes 3538952 | tf_op jit(solution)/shard_map/ppermute | solution.py:279
  103.9 3.6 %collective-permute-start.16 = (bf16[3,256,384]{2,1,0:T(8,128)(2,1)S(1)}, bf16[3,256,384]{2,1,0:T(8,128)(2,1)S(1)}, u32[]{:S(2)}, u32[]{:S(2)}) collective-permute-start(bf16[3,256,384]{2,1,0:T(8,128)(2,1)S(1)} %get-tuple-element.54), channel_id=1, source_target_pairs={{0,1},{1,0},{2,3},{3,2},{4,5},{5,4},{6,7},{7,6}} | collective-permute-start | bytes 1769480 | tf_op jit(solution)/shard_map/ppermute | solution.py:320
  104.3 28.3 %collective-permute-start.3 = (bf16[3,768,256]{2,1,0:T(8,128)(2,1)S(1)}, bf16[3,768,256]{2,1,0:T(8,128)(2,1)S(1)}, u32[]{:S(2)}, u32[]{:S(2)}) collective-permute-start(bf16[3,768,256]{2,1,0:T(8,128)(2,1)S(1)} %copy-done.3), channel_id=1, source_target_pairs={{0,2},{1,3},{2,0},{3,1},{4,6},{5,7},{6,4},{7,5}} | collective-permute-start | bytes 3538952 | tf_op jit(solution)/shard_map/ppermute | solution.py:218
  106.3 35.5 %collective-permute-start.2 = (bf16[3,768,256]{2,1,0:T(8,128)(2,1)S(1)}, bf16[3,768,256]{2,1,0:T(8,128)(2,1)S(1)}, u32[]{:S(2)}, u32[]{:S(2)}) collective-permute-start(bf16[3,768,256]{2,1,0:T(8,128)(2,1)S(1)} %copy-done.3), channel_id=1, source_target_pairs={{0,1},{1,0},{2,3},{3,2},{4,5},{5,4},{6,7},{7,6}} | collective-permute-start | bytes 3538952 | tf_op jit(solution)/shard_map/ppermute | solution.py:221
  110.7 22.4 %copy-start.2 = (bf16[3,768,256]{2,1,0:T(8,128)(2,1)S(1)}, bf16[3,768,256]{2,1,0:T(8,128)(2,1)}, u32[]{:S(2)}) copy-start(bf16[3,768,256]{2,1,0:T(8,128)(2,1)} %get-tuple-element.36.a0.a_ref) | copy-start | bytes 3538948
  132.6 9.2 %collective-permute-start.17 = (bf16[3,768,256]{2,1,0:T(8,128)(2,1)S(1)}, bf16[3,768,256]{2,1,0:T(8,128)(2,1)S(1)}, u32[]{:S(2)}, u32[]{:S(2)}) collective-permute-start(bf16[3,768,256]{2,1,0:T(8,128)(2,1)S(1)} %collective-permute-done.3.a2), channel_id=1, source_target_pairs={{0,1},{1,0},{2,3},{3,2},{4,5},{5,4},{6,7},{7,6}} | collective-permute-start | bytes 3538952 | tf_op jit(solution)/shard_map/ppermute | solution.py:279
  132.6 4.0 %collective-permute-start.18 = (bf16[4,256,384]{2,1,0:T(8,128)(2,1)S(1)}, bf16[4,256,384]{2,1,0:T(8,128)(2,1)S(1)}, u32[]{:S(2)}, u32[]{:S(2)}) collective-permute-start(bf16[4,256,384]{2,1,0:T(8,128)(2,1)S(1)} %get-tuple-element.59), channel_id=1, source_target_pairs={{0,1},{1,0},{2,3},{3,2},{4,5},{5,4},{6,7},{7,6}} | collective-permute-start | bytes 2359304 | tf_op jit(solution)/shard_map/ppermute | solution.py:320
  133.1 27.9 %collective-permute-start.1 = (bf16[3,768,256]{2,1,0:T(8,128)(2,1)S(1)}, bf16[3,768,256]{2,1,0:T(8,128)(2,1)S(1)}, u32[]{:S(2)}, u32[]{:S(2)}) collective-permute-start(bf16[3,768,256]{2,1,0:T(8,128)(2,1)S(1)} %copy-done.2), channel_id=1, source_target_pairs={{0,2},{1,3},{2,0},{3,1},{4,6},{5,7},{6,4},{7,5}} | collective-permute-start | bytes 3538952 | tf_op jit(solution)/shard_map/ppermute | solution.py:218
  134.8 26.7 %collective-permute-start = (bf16[3,768,256]{2,1,0:T(8,128)(2,1)S(1)}, bf16[3,768,256]{2,1,0:T(8,128)(2,1)S(1)}, u32[]{:S(2)}, u32[]{:S(2)}) collective-permute-start(bf16[3,768,256]{2,1,0:T(8,128)(2,1)S(1)} %copy-done.2), channel_id=1, source_target_pairs={{0,1},{1,0},{2,3},{3,2},{4,5},{5,4},{6,7},{7,6}} | collective-permute-start | bytes 3538952 | tf_op jit(solution)/shard_map/ppermute | solution.py:221
  161.0 2.8 %collective-permute-start.19 = (bf16[3,768,256]{2,1,0:T(8,128)(2,1)S(1)}, bf16[3,768,256]{2,1,0:T(8,128)(2,1)S(1)}, u32[]{:S(2)}, u32[]{:S(2)}) collective-permute-start(bf16[3,768,256]{2,1,0:T(8,128)(2,1)S(1)} %collective-permute-done.1.a2), channel_id=1, source_target_pairs={{0,1},{1,0},{2,3},{3,2},{4,5},{5,4},{6,7},{7,6}} | collective-permute-start | bytes 3538952 | tf_op jit(solution)/shard_map/ppermute | solution.py:279
  161.0 21.5 %collective-permute-start.22 = (bf16[3,256,384]{2,1,0:T(8,128)(2,1)S(1)}, bf16[3,256,384]{2,1,0:T(8,128)(2,1)S(1)}, u32[]{:S(2)}, u32[]{:S(2)}) collective-permute-start(bf16[3,256,384]{2,1,0:T(8,128)(2,1)S(1)} %get-tuple-element.66), channel_id=1, source_target_pairs={{0,1},{1,0},{2,3},{3,2},{4,5},{5,4},{6,7},{7,6}} | collective-permute-start | bytes 1769480 | tf_op jit(solution)/shard_map/ppermute | solution.py:320
  161.5 24.2 %collective-permute-start.21 = (bf16[3,256,384]{2,1,0:T(8,128)(2,1)S(1)}, bf16[3,256,384]{2,1,0:T(8,128)(2,1)S(1)}, u32[]{:S(2)}, u32[]{:S(2)}) collective-permute-start(bf16[3,256,384]{2,1,0:T(8,128)(2,1)S(1)} %get-tuple-element.65), channel_id=1, source_target_pairs={{0,1},{1,0},{2,3},{3,2},{4,5},{5,4},{6,7},{7,6}} | collective-permute-start | bytes 1769480 | tf_op jit(solution)/shard_map/ppermute | solution.py:320
  182.3 6.6 %collective-permute-start.20 = (bf16[3,256,384]{2,1,0:T(8,128)(2,1)S(1)}, bf16[3,256,384]{2,1,0:T(8,128)(2,1)S(1)}, u32[]{:S(2)}, u32[]{:S(2)}) collective-permute-start(bf16[3,256,384]{2,1,0:T(8,128)(2,1)S(1)} %get-tuple-element.64), channel_id=1, source_target_pairs={{0,1},{1,0},{2,3},{3,2},{4,5},{5,4},{6,7},{7,6}} | collective-permute-start | bytes 1769480 | tf_op jit(solution)/shard_map/ppermute | solution.py:320
  (8 other events, 79.2 us)
where the time goes:
time: 194 us; the launch traced here: 192 us
  Pallas kernels  135 us (70%)
  waiting for transfers between devices  38 us (20%)
  starting transfers between devices  10.5 us (5%)
  local copies, waits for them, and re-layouts  6.84 us (4%)
    pallas_call x5, Pallas kernels, local_block(): attn(idx, ctx_len, row_of[i], a_own[i], a_c[i], a_x[i], a_xc[i], tab, col...  101 us
    ppermute x5, waiting for transfers between devices, local_block(): a_x.append(lax.ppermute(a, 'sp', across_x))  26 us
    pallas_call x5, Pallas kernels, finish(): pl.pallas_call(dense_kernel, grid_spec=pltpu.PrefetchScalarGridSpec(num_s...  18 us
    pallas_call x2, Pallas kernels, norm(): pl.pallas_call(functools.partial(norm_kernel, plan), grid=(total // step_...  15.9 us
    ppermute x5, waiting for transfers between devices, fetch(): a_xc[i] = lax.ppermute(got[0], 'sp', across_core)  8.01 us
    ppermute x5, starting transfers between devices, local_block(): a_x.append(lax.ppermute(a, 'sp', across_x))  4.44 us
  transfers between devices with their start and end apart: 23, of which 10 were waited for; matrix products, arithmetic and copies ran while one was open for 3% of the time, Pallas kernels for 69%

commit v1 on v0

--- a/solution.py
+++ b/solution.py
@@ -12,7 +12,7 @@
 ROPE_BASE = 10000.0
 LN_EPS = 1e-5
 LOG2E = 1.4426950408889634
-CHUNKS = (3, 4, 3, 3, 3)
+CHUNKS = (4, 3, 3, 3, 3)
 F32 = jnp.float32
 BF16 = jnp.bfloat16
 
@@ -220,6 +220,7 @@
         for a in a_own:
             a_c.append(lax.ppermute(a, 'sp', across_core))
 
+        pos_ids, _ = lax.optimization_barrier((pos_ids, a_own[0]))
         last = pos_ids[:, blk - 1:].reshape(1, n_rows)
         last_x = lax.ppermute(last, 'sp', across_x)
         last_c = lax.ppermute(last, 'sp', across_core)
@@ -312,7 +313,7 @@
                 ),
                 out_shape=[kv_shape, kv_shape, c_shape, c_shape],
                 input_output_aliases={11: 0, 12: 1} if extra else {},
-                compiler_params=params(28),
+                compiler_params=params(22),
                 cost_estimate=pl.CostEstimate(flops=n * 6_000_000_000, bytes_accessed=n * 4_000_000, transcendentals=0),
                 name="attn",
             )

time: 194 us -> 193 us (level)
  Pallas kernels: 135 us -> 133 us
    ppermute x5, waiting for transfers between devices: 26 us -> 28.4 us  [local_block(): a_x.append(lax.ppermute(a, 'sp', across_x))]
  transfers between devices with their start and end apart: 23 -> 23, of which waited for: 10 -> 10; matrix products, arithmetic and copies ran while one was open for 3% -> 3% of each run, Pallas kernels for 69% -> 66%
where the time goes in v1:
time: 193 us; the launch traced here: 192 us
  Pallas kernels  133 us (69%)
  waiting for transfers between devices  39 us (20%)
  starting transfers between devices  11.8 us (6%)
  local copies, waits for them, and re-layouts  7.21 us (4%)
    pallas_call x5, Pallas kernels, local_block(): attn(idx, ctx_len, row_of[i], a_own[i], a_c[i], a_x[i], a_xc[i], tab, col...  100 us
    ppermute x5, waiting for transfers between devices, local_block(): a_x.append(lax.ppermute(a, 'sp', across_x))  28.4 us
    pallas_call x5, Pallas kernels, finish(): pl.pallas_call(dense_kernel, grid_spec=pltpu.PrefetchScalarGridSpec(num_s...  18 us
    pallas_call x2, Pallas kernels, norm(): pl.pallas_call(functools.partial(norm_kernel, plan), grid=(total // step_...  14.8 us
    ppermute x5, waiting for transfers between devices, fetch(): a_xc[i] = lax.ppermute(got[0], 'sp', across_core)  6.31 us
    ppermute x5, starting transfers between devices, local_block(): a_x.append(lax.ppermute(a, 'sp', across_x))  5.8 us
  transfers between devices with their start and end apart: 23, of which 10 were waited for; matrix products, arithmetic and copies ran while one was open for 3% of the time, Pallas kernels for 66%

profile of v1, /device:TPU:0, one launch (start us, length us, event | category | flops | bytes accessed | tf_op | source)
XLA Modules:
  0.0 192.3 jit_solution(16010956730540227429)
XLA Ops:
  0.7 3.5 %norm.3.a0.a_ref = bf16[4,768,256]{2,1,0:T(8,128)(2,1)} custom-call(bf16[16,256,768]{2,1,0:T(8,128)(2,1)} %h_ref.3, bf16[768]{0:T(1024)(128)(2,1)} %g_ref.3, bf16[768]{0:T(1024)(128)(2,1)} %b_ref.8), custom_call_target="tpu_custom_call" | custom-call | flops 2000000000 | bytes 3200000 | tf_op jit(solution)/shard_map/norm/pallas_call | solution.py:201
  4.4 3.3 %collective-permute-start.11 = (s32[1,16]{1,0:T(1,128)S(1)}, s32[1,16]{1,0:T(1,128)S(1)}, u32[]{:S(2)}, u32[]{:S(2)}) collective-permute-start(s32[1,16]{1,0:T(1,128)S(1)} %bitcast.54), channel_id=1, source_target_pairs={{0,2},{1,3},{2,0},{3,1},{4,6},{5,7},{6,4},{7,5}} | collective-permute-start | bytes 200 | tf_op jit(solution)/shard_map/ppermute | solution.py:225
  8.5 11.3 %norm.2 = (bf16[3,768,256]{2,1,0:T(8,128)(2,1)}, bf16[3,768,256]{2,1,0:T(8,128)(2,1)}, bf16[3,768,256]{2,1,0:T(8,128)(2,1)}, bf16[3,768,256]{2,1,0:T(8,128)(2,1)}) custom-call(bf16[16,256,768]{2,1,0:T(8,128)(2,1)} %h_ref.3, bf16[768]{0:T(1024)(128)(2,1)} %g_ref.3, bf16[768]{0:T(1024)(128)(2,1)} %b_ref.8), custom_call_target="tpu_custom_call" | custom-call | flops 6000000000 | bytes 9600000 | tf_op jit(solution)/shard_map/norm/pallas_call | solution.py:201
  20.0 1.1 collective-permute-done.12
  21.4 1.1 broadcast_in_dim.16.col_ref
  22.4 1.1 broadcast_in_dim.6.bias_ref
  23.5 2.2 %copy.37 = bf16[768,12,3,64]{0,3,1,2:T(8,128)(2,1)S(1)} copy(bf16[768,12,3,64]{0,3,2,1:T(8,128)(2,1)} %param.20) | data formatting | bytes 7077888 | tf_op jit(solution)/shard_map/optimization_barrier | solution.py:243
  25.9 18.9 %collective-permute-done.9.a2 = bf16[4,768,256]{2,1,0:T(8,128)(2,1)} collective-permute-done((bf16[4,768,256]{2,1,0:T(8,128)(2,1)}, bf16[4,768,256]{2,1,0:T(8,128)(2,1)}, u32[]{:S(2)}, u32[]{:S(2)}) %collective-permute-start.9) | collective-permute-done | bytes 1572896 | tf_op jit(solution)/shard_map/ppermute | solution.py:218
  45.4 3.1 %collective-permute-done.13.a3 = bf16[4,768,256]{2,1,0:T(8,128)(2,1)} collective-permute-done((bf16[4,768,256]{2,1,0:T(8,128)(2,1)}, bf16[4,768,256]{2,1,0:T(8,128)(2,1)}, u32[]{:S(2)}, u32[]{:S(2)}) %collective-permute-start.13) | collective-permute-done | bytes 1572896 | tf_op jit(solution)/shard_map/ppermute | solution.py:280
  48.6 1.1 copy-done.5
  49.7 1.0 copy-done.7
  50.7 25.1 %attn.5 = (bf16[16,192,1024]{2,1,0:T(8,128)(2,1)}, bf16[16,192,1024]{2,1,0:T(8,128)(2,1)}, bf16[4,256,384]{2,1,0:T(8,128)(2,1)S(1)}, bf16[4,256,384]{2,1,0:T(8,128)(2,1)S(1)}) custom-call(s32[9]{0:T(128)S(1)} %stack.52.idx_ref, s32[16]{0:T(128)S(1)} %copy-done.10, s32[1]{0:T(128)} %constant.15.clone.1.row_ref, bf16[4,768,256]{2,1,0:T(8,128)(2,1)S(1)} %copy-done.1, ...), custom_call_target="tpu_custom_call" | custom-call | flops 24000000000 | bytes 16000000 | tf_op jit(solution)/shard_map/attn/pallas_call | solution.py:320
  76.0 2.0 %collective-permute-start.5 = (bf16[3,768,256]{2,1,0:T(8,128)(2,1)S(1)}, bf16[3,768,256]{2,1,0:T(8,128)(2,1)S(1)}, u32[]{:S(2)}, u32[]{:S(2)}) collective-permute-start(bf16[3,768,256]{2,1,0:T(8,128)(2,1)S(1)} %copy-done.4), channel_id=1, source_target_pairs={{0,2},{1,3},{2,0},{3,1},{4,6},{5,7},{6,4},{7,5}} | collective-permute-start | bytes 3538952 | tf_op jit(solution)/shard_map/ppermute | solution.py:218
  78.1 0.8 collective-permute-done.14.a3
  78.9 19.7 %attn.6 = (bf16[16,192,1024]{2,1,0:T(8,128)(2,1)}, bf16[16,192,1024]{2,1,0:T(8,128)(2,1)}, bf16[3,256,384]{2,1,0:T(8,128)(2,1)S(1)}, bf16[3,256,384]{2,1,0:T(8,128)(2,1)S(1)}) custom-call(s32[9]{0:T(128)S(1)} %stack.52.idx_ref, s32[16]{0:T(128)S(1)} %copy-done.10, s32[1]{0:T(128)} %constant.14.clone.1.row_ref, ...), custom_call_target="tpu_custom_call", output_to_operand_aliasing={{0}: (11, {}), {1}: (12, {})} | custom-call | flops 17999998976 | bytes 12000000 | tf_op jit(solution)/shard_map/attn/pallas_call | solution.py:320
  98.7 5.8 %collective-permute-done.5.a2 = bf16[3,768,256]{2,1,0:T(8,128)(2,1)S(1)} collective-permute-done((bf16[3,768,256]{2,1,0:T(8,128)(2,1)S(1)}, bf16[3,768,256]{2,1,0:T(8,128)(2,1)S(1)}, u32[]{:S(2)}, u32[]{:S(2)}) %collective-permute-start.5) | collective-permute-done | bytes 1179680 | tf_op jit(solution)/shard_map/ppermute | solution.py:218
  105.0 1.7 collective-permute-start.3
  106.7 1.7 collective-permute-done.16.other_ref
  108.5 3.8 %dense.5.rest_0_ = bf16[16,256,768]{2,1,0:T(8,128)(2,1)} custom-call(s32[9]{0:T(128)S(1)} %stack.52.idx_ref, s32[1]{0:T(128)} %constant.15.clone.1.row_ref, bf16[4,256,384]{2,1,0:T(8,128)(2,1)S(1)} %get-tuple-element.47.own_ref, bf16[4,256,384]{2,1,0:T(8,128)(2,1)S(1)} %collective-permute-done.16.other_ref, bf16[4,768,256]{2,1,0:T(8,128)(2,1)S(1)} %copy-done.1, ...), custom_call_target="tpu_custom_call" | custom-call | flops 4000000000 | bytes 8000000 | tf_op jit(solution)/shard_map/dense/pallas_call | solution.py:256
  112.3 18.4 %attn.7 = (bf16[16,192,1024]{2,1,0:T(8,128)(2,1)}, bf16[16,192,1024]{2,1,0:T(8,128)(2,1)}, bf16[3,256,384]{2,1,0:T(8,128)(2,1)S(1)}, bf16[3,256,384]{2,1,0:T(8,128)(2,1)S(1)}) custom-call(s32[9]{0:T(128)S(1)} %stack.52.idx_ref, s32[16]{0:T(128)S(1)} %copy-done.10, s32[1]{0:T(128)} %constant.13.clone.1.row_ref, ...), custom_call_target="tpu_custom_call", output_to_operand_aliasing={{0}: (11, {}), {1}: (12, {})} | custom-call | flops 17999998976 | bytes 12000000 | tf_op jit(solution)/shard_map/attn/pallas_call | solution.py:320
  130.7 2.2 %collective-permute-done.3.a2 = bf16[3,768,256]{2,1,0:T(8,128)(2,1)S(1)} collective-permute-done((bf16[3,768,256]{2,1,0:T(8,128)(2,1)S(1)}, bf16[3,768,256]{2,1,0:T(8,128)(2,1)S(1)}, u32[]{:S(2)}, u32[]{:S(2)}) %collective-permute-start.3) | collective-permute-done | bytes 1179680 | tf_op jit(solution)/shard_map/ppermute | solution.py:218
  133.4 1.7 collective-permute-start.1
  135.1 1.4 collective-permute-done.18.other_ref
  136.6 4.6 %dense.6.rest_0_ = bf16[16,256,768]{2,1,0:T(8,128)(2,1)} custom-call(s32[9]{0:T(128)S(1)} %stack.52.idx_ref, s32[1]{0:T(128)} %constant.14.clone.1.row_ref, bf16[3,256,384]{2,1,0:T(8,128)(2,1)S(1)} %get-tuple-element.51.own_ref, bf16[3,256,384]{2,1,0:T(8,128)(2,1)S(1)} %collective-permute-done.18.other_ref, ...), custom_call_target="tpu_custom_call", output_to_operand_aliasing={{}: (10, {})} | custom-call | flops 3000000000 | bytes 6000000 | tf_op jit(solution)/shard_map/dense/pallas_call | solution.py:256
  141.2 18.6 %attn.8 = (bf16[16,192,1024]{2,1,0:T(8,128)(2,1)}, bf16[16,192,1024]{2,1,0:T(8,128)(2,1)}, bf16[3,256,384]{2,1,0:T(8,128)(2,1)S(1)}, bf16[3,256,384]{2,1,0:T(8,128)(2,1)S(1)}) custom-call(s32[9]{0:T(128)S(1)} %stack.52.idx_ref, s32[16]{0:T(128)S(1)} %copy-done.10, s32[1]{0:T(128)} %constant.21.clone.1.row_ref, ...), custom_call_target="tpu_custom_call", output_to_operand_aliasing={{0}: (11, {}), {1}: (12, {})} | custom-call | flops 17999998976 | bytes 12000000 | tf_op jit(solution)/shard_map/attn/pallas_call | solution.py:320
  159.8 1.5 collective-permute-done.1.a2
  161.3 0.5 collective-permute-start.22
  161.8 2.3 %collective-permute-done.19.a3 = bf16[3,768,256]{2,1,0:T(8,128)(2,1)S(1)} collective-permute-done((bf16[3,768,256]{2,1,0:T(8,128)(2,1)S(1)}, bf16[3,768,256]{2,1,0:T(8,128)(2,1)S(1)}, u32[]{:S(2)}, u32[]{:S(2)}) %collective-permute-start.19) | collective-permute-done | bytes 1179680 | tf_op jit(solution)/shard_map/ppermute | solution.py:280
  164.1 18.4 %attn.9 = (bf16[16,192,1024]{2,1,0:T(8,128)(2,1)}, bf16[16,192,1024]{2,1,0:T(8,128)(2,1)}, bf16[3,256,384]{2,1,0:T(8,128)(2,1)S(1)}, bf16[3,256,384]{2,1,0:T(8,128)(2,1)S(1)}) custom-call(s32[9]{0:T(128)S(1)} %stack.52.idx_ref, s32[16]{0:T(128)S(1)} %copy-done.10, s32[1]{0:T(128)} %constant.20.clone.1.row_ref, ...), custom_call_target="tpu_custom_call", output_to_operand_aliasing={{0}: (11, {}), {1}: (12, {})} | custom-call | flops 17999998976 | bytes 12000000 | tf_op jit(solution)/shard_map/attn/pallas_call | solution.py:320
  182.6 3.2 %dense.7.rest_0_ = bf16[16,256,768]{2,1,0:T(8,128)(2,1)} custom-call(s32[9]{0:T(128)S(1)} %stack.52.idx_ref, s32[1]{0:T(128)} %constant.13.clone.1.row_ref, bf16[3,256,384]{2,1,0:T(8,128)(2,1)S(1)} %get-tuple-element.55.own_ref, bf16[3,256,384]{2,1,0:T(8,128)(2,1)S(1)} %collective-permute-done.22.other_ref, ...), custom_call_target="tpu_custom_call", output_to_operand_aliasing={{}: (10, {})} | custom-call | flops 3000000000 | bytes 6000000 | tf_op jit(solution)/shard_map/dense/pallas_call | solution.py:256
  185.9 3.2 %dense.8.rest_0_ = bf16[16,256,768]{2,1,0:T(8,128)(2,1)} custom-call(s32[9]{0:T(128)S(1)} %stack.52.idx_ref, s32[1]{0:T(128)} %constant.21.clone.1.row_ref, bf16[3,256,384]{2,1,0:T(8,128)(2,1)S(1)} %get-tuple-element.60.own_ref, bf16[3,256,384]{2,1,0:T(8,128)(2,1)S(1)} %collective-permute-done.21.other_ref, ...), custom_call_target="tpu_custom_call", output_to_operand_aliasing={{}: (10, {})} | custom-call | flops 3000000000 | bytes 6000000 | tf_op jit(solution)/shard_map/dense/pallas_call | solution.py:256
  189.1 3.2 %dense.9 = bf16[16,256,768]{2,1,0:T(8,128)(2,1)} custom-call(s32[9]{0:T(128)S(1)} %stack.52.idx_ref, s32[1]{0:T(128)} %constant.20.clone.1.row_ref, bf16[3,256,384]{2,1,0:T(8,128)(2,1)S(1)} %get-tuple-element.65.own_ref, bf16[3,256,384]{2,1,0:T(8,128)(2,1)S(1)} %collective-permute-done.20.other_ref, ...), custom_call_target="tpu_custom_call", output_to_operand_aliasing={{}: (10, {})} | custom-call | flops 3000000000 | bytes 6000000 | tf_op jit(solution)/shard_map/dense/pallas_call | solution.py:256
  (81 shorter events, 3.6 us)
Async XLA Ops:
  4.4 15.5 %collective-permute-start.11 = (s32[1,16]{1,0:T(1,128)S(1)}, s32[1,16]{1,0:T(1,128)S(1)}, u32[]{:S(2)}, u32[]{:S(2)}) collective-permute-start(s32[1,16]{1,0:T(1,128)S(1)} %bitcast.54), channel_id=1, source_target_pairs={{0,2},{1,3},{2,0},{3,1},{4,6},{5,7},{6,4},{7,5}} | collective-permute-start | bytes 200 | tf_op jit(solution)/shard_map/ppermute | solution.py:225
  7.7 12.3 %collective-permute-start.10 = (s32[1,16]{1,0:T(1,128)S(1)}, s32[1,16]{1,0:T(1,128)S(1)}, u32[]{:S(2)}, u32[]{:S(2)}) collective-permute-start(s32[1,16]{1,0:T(1,128)S(1)} %bitcast.55), channel_id=1, source_target_pairs={{0,1},{1,0},{2,3},{3,2},{4,5},{5,4},{6,7},{7,6}} | collective-permute-start | bytes 200 | tf_op jit(solution)/shard_map/ppermute | solution.py:226
  7.7 37.1 %collective-permute-start.9 = (bf16[4,768,256]{2,1,0:T(8,128)(2,1)}, bf16[4,768,256]{2,1,0:T(8,128)(2,1)}, u32[]{:S(2)}, u32[]{:S(2)}) collective-permute-start(bf16[4,768,256]{2,1,0:T(8,128)(2,1)} %norm.3.a0.a_ref), channel_id=1, source_target_pairs={{0,2},{1,3},{2,0},{3,1},{4,6},{5,7},{6,4},{7,5}} | collective-permute-start | bytes 4718600 | tf_op jit(solution)/shard_map/ppermute | solution.py:218
  7.8 37.7 %collective-permute-start.8 = (bf16[4,768,256]{2,1,0:T(8,128)(2,1)}, bf16[4,768,256]{2,1,0:T(8,128)(2,1)}, u32[]{:S(2)}, u32[]{:S(2)}) collective-permute-start(bf16[4,768,256]{2,1,0:T(8,128)(2,1)} %norm.3.a0.a_ref), channel_id=1, source_target_pairs={{0,1},{1,0},{2,3},{3,2},{4,5},{5,4},{6,7},{7,6}} | collective-permute-start | bytes 4718600 | tf_op jit(solution)/shard_map/ppermute | solution.py:221
  8.5 12.6 %copy-start.17 = (f32[16]{0:T(128)S(1)}, f32[16]{0:T(128)}, u32[]{:S(2)}) copy-start(f32[16]{0:T(128)} %constant.42.clone) | copy-start | bytes 196
  19.9 1.2 collective-permute-start.12
  25.7 22.8 %copy-start.1 = (bf16[4,768,256]{2,1,0:T(8,128)(2,1)S(1)}, bf16[4,768,256]{2,1,0:T(8,128)(2,1)}, u32[]{:S(2)}) copy-start(bf16[4,768,256]{2,1,0:T(8,128)(2,1)} %norm.3.a0.a_ref) | copy-start | bytes 4718596
  44.8 3.8 %collective-permute-start.13 = (bf16[4,768,256]{2,1,0:T(8,128)(2,1)}, bf16[4,768,256]{2,1,0:T(8,128)(2,1)}, u32[]{:S(2)}, u32[]{:S(2)}) collective-permute-start(bf16[4,768,256]{2,1,0:T(8,128)(2,1)} %collective-permute-done.9.a2), channel_id=1, source_target_pairs={{0,1},{1,0},{2,3},{3,2},{4,5},{5,4},{6,7},{7,6}} | collective-permute-start | bytes 4718600 | tf_op jit(solution)/shard_map/ppermute | solution.py:280
  44.8 31.0 %collective-permute-start.7 = (bf16[3,768,256]{2,1,0:T(8,128)(2,1)}, bf16[3,768,256]{2,1,0:T(8,128)(2,1)}, u32[]{:S(2)}, u32[]{:S(2)}) collective-permute-start(bf16[3,768,256]{2,1,0:T(8,128)(2,1)} %get-tuple-element.40.a0.a_ref), channel_id=1, source_target_pairs={{0,2},{1,3},{2,0},{3,1},{4,6},{5,7},{6,4},{7,5}} | collective-permute-start | bytes 3538952 | tf_op jit(solution)/shard_map/ppermute | solution.py:218
  45.1 32.9 %collective-permute-start.6 = (bf16[3,768,256]{2,1,0:T(8,128)(2,1)}, bf16[3,768,256]{2,1,0:T(8,128)(2,1)}, u32[]{:S(2)}, u32[]{:S(2)}) collective-permute-start(bf16[3,768,256]{2,1,0:T(8,128)(2,1)} %get-tuple-element.40.a0.a_ref), channel_id=1, source_target_pairs={{0,1},{1,0},{2,3},{3,2},{4,5},{5,4},{6,7},{7,6}} | collective-permute-start | bytes 3538952 | tf_op jit(solution)/shard_map/ppermute | solution.py:221
  45.4 30.5 %copy-start.4 = (bf16[3,768,256]{2,1,0:T(8,128)(2,1)S(1)}, bf16[3,768,256]{2,1,0:T(8,128)(2,1)}, u32[]{:S(2)}) copy-start(bf16[3,768,256]{2,1,0:T(8,128)(2,1)} %get-tuple-element.39.a0.a_ref) | copy-start | bytes 3538948
  50.7 28.2 %copy-start.6 = (f32[1152,128]{1,0:T(8,128)S(1)}, f32[1152,128]{1,0:T(8,128)}, u32[]{:S(2)}) copy-start(f32[1152,128]{1,0:T(8,128)} %broadcast_in_dim.6.bias_ref) | copy-start | bytes 1769476
  50.7 28.2 %copy-start.8 = (f32[16,64,128]{2,1,0:T(8,128)S(1)}, f32[16,64,128]{2,1,0:T(8,128)}, u32[]{:S(2)}) copy-start(f32[16,64,128]{2,1,0:T(8,128)} %broadcast_in_dim.16.col_ref) | copy-start | bytes 1572868
  75.8 3.1 %collective-permute-start.14 = (bf16[3,768,256]{2,1,0:T(8,128)(2,1)}, bf16[3,768,256]{2,1,0:T(8,128)(2,1)S(1)}, u32[]{:S(2)}, u32[]{:S(2)}) collective-permute-start(bf16[3,768,256]{2,1,0:T(8,128)(2,1)} %collective-permute-done.7.a2), channel_id=1, source_target_pairs={{0,1},{1,0},{2,3},{3,2},{4,5},{5,4},{6,7},{7,6}} | collective-permute-start | bytes 3538952 | tf_op jit(solution)/shard_map/ppermute | solution.py:280
  76.0 28.5 %collective-permute-start.5 = (bf16[3,768,256]{2,1,0:T(8,128)(2,1)S(1)}, bf16[3,768,256]{2,1,0:T(8,128)(2,1)S(1)}, u32[]{:S(2)}, u32[]{:S(2)}) collective-permute-start(bf16[3,768,256]{2,1,0:T(8,128)(2,1)S(1)} %copy-done.4), channel_id=1, source_target_pairs={{0,2},{1,3},{2,0},{3,1},{4,6},{5,7},{6,4},{7,5}} | collective-permute-start | bytes 3538952 | tf_op jit(solution)/shard_map/ppermute | solution.py:218
  77.9 34.3 %collective-permute-start.4 = (bf16[3,768,256]{2,1,0:T(8,128)(2,1)S(1)}, bf16[3,768,256]{2,1,0:T(8,128)(2,1)S(1)}, u32[]{:S(2)}, u32[]{:S(2)}) collective-permute-start(bf16[3,768,256]{2,1,0:T(8,128)(2,1)S(1)} %copy-done.4), channel_id=1, source_target_pairs={{0,1},{1,0},{2,3},{3,2},{4,5},{5,4},{6,7},{7,6}} | collective-permute-start | bytes 3538952 | tf_op jit(solution)/shard_map/ppermute | solution.py:221
  78.9 26.1 %copy-start.3 = (bf16[3,768,256]{2,1,0:T(8,128)(2,1)S(1)}, bf16[3,768,256]{2,1,0:T(8,128)(2,1)}, u32[]{:S(2)}) copy-start(bf16[3,768,256]{2,1,0:T(8,128)(2,1)} %get-tuple-element.38.a0.a_ref) | copy-start | bytes 3538948
  78.9 29.5 %copy-start = (bf16[768,768]{1,0:T(8,128)(2,1)S(1)}, bf16[768,768]{1,0:T(8,128)(2,1)}, u32[]{:S(2)}) copy-start(bf16[768,768]{1,0:T(8,128)(2,1)} %param.22) | copy-start | bytes 3538948
  78.9 29.5 %copy-start.9 = (bf16[768]{0:T(1024)(128)(2,1)S(1)}, bf16[768]{0:T(1024)(128)(2,1)}, u32[]{:S(2)}) copy-start(bf16[768]{0:T(1024)(128)(2,1)} %b_ref.13) | copy-start | bytes 4612
  104.5 7.8 %collective-permute-start.15 = (bf16[3,768,256]{2,1,0:T(8,128)(2,1)S(1)}, bf16[3,768,256]{2,1,0:T(8,128)(2,1)S(1)}, u32[]{:S(2)}, u32[]{:S(2)}) collective-permute-start(bf16[3,768,256]{2,1,0:T(8,128)(2,1)S(1)} %collective-permute-done.5.a2), channel_id=1, source_target_pairs={{0,1},{1,0},{2,3},{3,2},{4,5},{5,4},{6,7},{7,6}} | collective-permute-start | bytes 3538952 | tf_op jit(solution)/shard_map/ppermute | solution.py:280
  104.5 4.0 %collective-permute-start.16 = (bf16[4,256,384]{2,1,0:T(8,128)(2,1)S(1)}, bf16[4,256,384]{2,1,0:T(8,128)(2,1)S(1)}, u32[]{:S(2)}, u32[]{:S(2)}) collective-permute-start(bf16[4,256,384]{2,1,0:T(8,128)(2,1)S(1)} %get-tuple-element.56), channel_id=1, source_target_pairs={{0,1},{1,0},{2,3},{3,2},{4,5},{5,4},{6,7},{7,6}} | collective-permute-start | bytes 2359304 | tf_op jit(solution)/shard_map/ppermute | solution.py:321
  105.0 27.9 %collective-permute-start.3 = (bf16[3,768,256]{2,1,0:T(8,128)(2,1)S(1)}, bf16[3,768,256]{2,1,0:T(8,128)(2,1)S(1)}, u32[]{:S(2)}, u32[]{:S(2)}) collective-permute-start(bf16[3,768,256]{2,1,0:T(8,128)(2,1)S(1)} %copy-done.3), channel_id=1, source_target_pairs={{0,2},{1,3},{2,0},{3,1},{4,6},{5,7},{6,4},{7,5}} | collective-permute-start | bytes 3538952 | tf_op jit(solution)/shard_map/ppermute | solution.py:218
  106.7 34.4 %collective-permute-start.2 = (bf16[3,768,256]{2,1,0:T(8,128)(2,1)S(1)}, bf16[3,768,256]{2,1,0:T(8,128)(2,1)S(1)}, u32[]{:S(2)}, u32[]{:S(2)}) collective-permute-start(bf16[3,768,256]{2,1,0:T(8,128)(2,1)S(1)} %copy-done.3), channel_id=1, source_target_pairs={{0,1},{1,0},{2,3},{3,2},{4,5},{5,4},{6,7},{7,6}} | collective-permute-start | bytes 3538952 | tf_op jit(solution)/shard_map/ppermute | solution.py:221
  112.3 21.1 %copy-start.2 = (bf16[3,768,256]{2,1,0:T(8,128)(2,1)S(1)}, bf16[3,768,256]{2,1,0:T(8,128)(2,1)}, u32[]{:S(2)}) copy-start(bf16[3,768,256]{2,1,0:T(8,128)(2,1)} %get-tuple-element.37.a0.a_ref) | copy-start | bytes 3538948
  132.9 8.3 %collective-permute-start.17 = (bf16[3,768,256]{2,1,0:T(8,128)(2,1)S(1)}, bf16[3,768,256]{2,1,0:T(8,128)(2,1)S(1)}, u32[]{:S(2)}, u32[]{:S(2)}) collective-permute-start(bf16[3,768,256]{2,1,0:T(8,128)(2,1)S(1)} %collective-permute-done.3.a2), channel_id=1, source_target_pairs={{0,1},{1,0},{2,3},{3,2},{4,5},{5,4},{6,7},{7,6}} | collective-permute-start | bytes 3538952 | tf_op jit(solution)/shard_map/ppermute | solution.py:280
  132.9 3.7 %collective-permute-start.18 = (bf16[3,256,384]{2,1,0:T(8,128)(2,1)S(1)}, bf16[3,256,384]{2,1,0:T(8,128)(2,1)S(1)}, u32[]{:S(2)}, u32[]{:S(2)}) collective-permute-start(bf16[3,256,384]{2,1,0:T(8,128)(2,1)S(1)} %get-tuple-element.61), channel_id=1, source_target_pairs={{0,1},{1,0},{2,3},{3,2},{4,5},{5,4},{6,7},{7,6}} | collective-permute-start | bytes 1769480 | tf_op jit(solution)/shard_map/ppermute | solution.py:321
  133.4 27.9 %collective-permute-start.1 = (bf16[3,768,256]{2,1,0:T(8,128)(2,1)S(1)}, bf16[3,768,256]{2,1,0:T(8,128)(2,1)S(1)}, u32[]{:S(2)}, u32[]{:S(2)}) collective-permute-start(bf16[3,768,256]{2,1,0:T(8,128)(2,1)S(1)} %copy-done.2), channel_id=1, source_target_pairs={{0,2},{1,3},{2,0},{3,1},{4,6},{5,7},{6,4},{7,5}} | collective-permute-start | bytes 3538952 | tf_op jit(solution)/shard_map/ppermute | solution.py:218
  135.1 26.7 %collective-permute-start = (bf16[3,768,256]{2,1,0:T(8,128)(2,1)S(1)}, bf16[3,768,256]{2,1,0:T(8,128)(2,1)S(1)}, u32[]{:S(2)}, u32[]{:S(2)}) collective-permute-start(bf16[3,768,256]{2,1,0:T(8,128)(2,1)S(1)} %copy-done.2), channel_id=1, source_target_pairs={{0,1},{1,0},{2,3},{3,2},{4,5},{5,4},{6,7},{7,6}} | collective-permute-start | bytes 3538952 | tf_op jit(solution)/shard_map/ppermute | solution.py:221
  161.3 2.8 %collective-permute-start.19 = (bf16[3,768,256]{2,1,0:T(8,128)(2,1)S(1)}, bf16[3,768,256]{2,1,0:T(8,128)(2,1)S(1)}, u32[]{:S(2)}, u32[]{:S(2)}) collective-permute-start(bf16[3,768,256]{2,1,0:T(8,128)(2,1)S(1)} %collective-permute-done.1.a2), channel_id=1, source_target_pairs={{0,1},{1,0},{2,3},{3,2},{4,5},{5,4},{6,7},{7,6}} | collective-permute-start | bytes 3538952 | tf_op jit(solution)/shard_map/ppermute | solution.py:280
  161.3 21.4 %collective-permute-start.22 = (bf16[3,256,384]{2,1,0:T(8,128)(2,1)S(1)}, bf16[3,256,384]{2,1,0:T(8,128)(2,1)S(1)}, u32[]{:S(2)}, u32[]{:S(2)}) collective-permute-start(bf16[3,256,384]{2,1,0:T(8,128)(2,1)S(1)} %get-tuple-element.68), channel_id=1, source_target_pairs={{0,1},{1,0},{2,3},{3,2},{4,5},{5,4},{6,7},{7,6}} | collective-permute-start | bytes 1769480 | tf_op jit(solution)/shard_map/ppermute | solution.py:321
  161.8 24.1 %collective-permute-start.21 = (bf16[3,256,384]{2,1,0:T(8,128)(2,1)S(1)}, bf16[3,256,384]{2,1,0:T(8,128)(2,1)S(1)}, u32[]{:S(2)}, u32[]{:S(2)}) collective-permute-start(bf16[3,256,384]{2,1,0:T(8,128)(2,1)S(1)} %get-tuple-element.67), channel_id=1, source_target_pairs={{0,1},{1,0},{2,3},{3,2},{4,5},{5,4},{6,7},{7,6}} | collective-permute-start | bytes 1769480 | tf_op jit(solution)/shard_map/ppermute | solution.py:321
  182.5 6.6 %collective-permute-start.20 = (bf16[3,256,384]{2,1,0:T(8,128)(2,1)S(1)}, bf16[3,256,384]{2,1,0:T(8,128)(2,1)S(1)}, u32[]{:S(2)}, u32[]{:S(2)}) collective-permute-start(bf16[3,256,384]{2,1,0:T(8,128)(2,1)S(1)} %get-tuple-element.66), channel_id=1, source_target_pairs={{0,1},{1,0},{2,3},{3,2},{4,5},{5,4},{6,7},{7,6}} | collective-permute-start | bytes 1769480 | tf_op jit(solution)/shard_map/ppermute | solution.py:321
  (9 other events, 51.9 us)

commit v2 on v1

--- a/solution.py
+++ b/solution.py
@@ -12,7 +12,7 @@
 ROPE_BASE = 10000.0
 LN_EPS = 1e-5
 LOG2E = 1.4426950408889634
-CHUNKS = (4, 3, 3, 3, 3)
+CHUNKS = (4, 4, 3, 3, 2)
 F32 = jnp.float32
 BF16 = jnp.bfloat16
 
@@ -68,7 +68,7 @@
     blk = a0.shape[2]
     ctx = ctx_ref[row_ref[0] + pl.program_id(0)]
 
-    col = [jnp.concatenate([col_ref[0, 16 * i:16 * i + 16]] * 2, axis=1) for i in range(4)]
+    col = [jnp.concatenate([col_ref[16 * i:16 * i + 16]] * 2, axis=1) for i in range(4)]
     for m, a_ref in enumerate((a0, a1, a2, a3)):
         j = idx_ref[m]
         a = a_ref[0]
@@ -240,7 +240,8 @@
         bias = b_qkv.transpose(1, 0, 2).reshape(3, 2, 2, half)
         bias = lax.dynamic_index_in_dim(bias, core, 2, keepdims=False).reshape(3 * rows, 1)
         bias = jnp.broadcast_to(bias.astype(F32), (3 * rows, 128))
-        w, bias, col, tab = lax.optimization_barrier((w_qkv, bias, col, tab))
+        aux = jnp.concatenate([bias, col.reshape(n_rows * 64, 128)], axis=0)
+        w, aux, tab = lax.optimization_barrier((w_qkv, aux, tab))
         w = w.transpose(2, 1, 3, 0).reshape(3, 2, 2, half, width)
         w = lax.dynamic_index_in_dim(w, core, 2, keepdims=False).reshape(3 * rows, width)
         wd = w_dense.reshape(4, half, width)
@@ -279,7 +280,7 @@
             got = lax.optimization_barrier((a_x[i], *after))
             a_xc[i] = lax.ppermute(got[0], 'sp', across_core)
 
-        fetch(0, (a_own[1], w, bias, col))
+        fetch(0, (a_own[1], w, aux))
         pending = []
         for i, n in enumerate(CHUNKS):
             extra = [] if keys is None else [keys, values]
@@ -295,7 +296,7 @@
                     grid=(n,),
                     in_specs=[a_spec] * 4 + [
                         pl.BlockSpec((4, 32, blk), lambda b, *_: (0, 0, 0)),
-                        pl.BlockSpec((1, 64, 128), lambda b, i, c, r: (r[0] + b, 0, 0)),
+                        pl.BlockSpec((64, 128), lambda b, i, c, r: (3 * rows // 64 + r[0] + b, 0)),
                         pl.BlockSpec((3 * rows, width), lambda b, *_: (0, 0)),
                         pl.BlockSpec((3 * rows, 128), lambda b, *_: (0, 0))]
                     + [pl.BlockSpec(memory_space=pl.ANY)] * len(extra),
@@ -317,7 +318,7 @@
                 cost_estimate=pl.CostEstimate(flops=n * 6_000_000_000, bytes_accessed=n * 4_000_000, transcendentals=0),
                 name="attn",
             )
-            keys, values, own, send = attn(idx, ctx_len, row_of[i], a_own[i], a_c[i], a_x[i], a_xc[i], tab, col, w, bias, *extra)
+            keys, values, own, send = attn(idx, ctx_len, row_of[i], a_own[i], a_c[i], a_x[i], a_xc[i], tab, aux, w, aux, *extra)
             other = lax.ppermute(send, 'sp', across_core)
             if i + 1 < len(CHUNKS):
                 fetch(i + 1, (own,) + (() if out is None else (out,)))

time: 193 us -> 193 us (level)
  waiting for transfers between devices: 39 us -> 41.5 us
  transfers between devices with their start and end apart: 23 -> 23, of which waited for: 10 -> 9; matrix products, arithmetic and copies ran while one was open for 3% -> 2% of each run, Pallas kernels for 66% -> 66%
where the time goes in v2:
time: 193 us; the launch traced here: 192 us
  Pallas kernels  133 us (69%)
  waiting for transfers between devices  41.5 us (22%)
  starting transfers between devices  10.5 us (5%)
  local copies, waits for them, and re-layouts  5.65 us (3%)
    pallas_call x5, Pallas kernels, local_block(): attn(idx, ctx_len, row_of[i], a_own[i], a_c[i], a_x[i], a_xc[i], tab, aux...  100 us
    ppermute x5, waiting for transfers between devices, local_block(): a_x.append(lax.ppermute(a, 'sp', across_x))  29.3 us
    pallas_call x5, Pallas kernels, finish(): pl.pallas_call(dense_kernel, grid_spec=pltpu.PrefetchScalarGridSpec(num_s...  17.9 us
    pallas_call x2, Pallas kernels, norm(): pl.pallas_call(functools.partial(norm_kernel, plan), grid=(total // step_...  14.7 us
    ppermute x5, waiting for transfers between devices, fetch(): a_xc[i] = lax.ppermute(got[0], 'sp', across_core)  7.88 us
    ppermute x5, starting transfers between devices, local_block(): a_x.append(lax.ppermute(a, 'sp', across_x))  4.38 us
  transfers between devices with their start and end apart: 23, of which 9 were waited for; matrix products, arithmetic and copies ran while one was open for 2% of the time, Pallas kernels for 66%

profile of v2, /device:TPU:0, one launch (start us, length us, event | category | flops | bytes accessed | tf_op | source)
XLA Modules:
  0.0 191.6 jit_solution(5296728115760844707)
XLA Ops:
  0.7 3.5 %norm.3.a0.a_ref = bf16[4,768,256]{2,1,0:T(8,128)(2,1)} custom-call(bf16[16,256,768]{2,1,0:T(8,128)(2,1)} %h_ref.3, bf16[768]{0:T(1024)(128)(2,1)} %g_ref.3, bf16[768]{0:T(1024)(128)(2,1)} %b_ref.8), custom_call_target="tpu_custom_call" | custom-call | flops 2000000000 | bytes 3200000 | tf_op jit(solution)/shard_map/norm/pallas_call | solution.py:201
  4.4 3.3 %collective-permute-start.11 = (s32[1,16]{1,0:T(1,128)S(1)}, s32[1,16]{1,0:T(1,128)S(1)}, u32[]{:S(2)}, u32[]{:S(2)}) collective-permute-start(s32[1,16]{1,0:T(1,128)S(1)} %bitcast.54), channel_id=1, source_target_pairs={{0,2},{1,3},{2,0},{3,1},{4,6},{5,7},{6,4},{7,5}} | collective-permute-start | bytes 200 | tf_op jit(solution)/shard_map/ppermute | solution.py:225
  7.8 0.4 collective-permute-start.8
  8.5 11.2 %norm.2 = (bf16[4,768,256]{2,1,0:T(8,128)(2,1)}, bf16[3,768,256]{2,1,0:T(8,128)(2,1)}, bf16[3,768,256]{2,1,0:T(8,128)(2,1)}, bf16[2,768,256]{2,1,0:T(8,128)(2,1)}) custom-call(bf16[16,256,768]{2,1,0:T(8,128)(2,1)} %h_ref.3, bf16[768]{0:T(1024)(128)(2,1)} %g_ref.3, bf16[768]{0:T(1024)(128)(2,1)} %b_ref.8), custom_call_target="tpu_custom_call" | custom-call | flops 6000000000 | bytes 9600000 | tf_op jit(solution)/shard_map/norm/pallas_call | solution.py:201
  19.9 1.1 collective-permute-done.12
  21.3 1.4 broadcast.33.col_ref.bias_ref
  22.7 2.2 %copy.37 = bf16[768,12,3,64]{0,3,1,2:T(8,128)(2,1)S(1)} copy(bf16[768,12,3,64]{0,3,2,1:T(8,128)(2,1)} %param.20) | data formatting | bytes 7077888 | tf_op jit(solution)/shard_map/optimization_barrier | solution.py:244
  25.1 19.7 %collective-permute-done.9.a2 = bf16[4,768,256]{2,1,0:T(8,128)(2,1)} collective-permute-done((bf16[4,768,256]{2,1,0:T(8,128)(2,1)}, bf16[4,768,256]{2,1,0:T(8,128)(2,1)}, u32[]{:S(2)}, u32[]{:S(2)}) %collective-permute-start.9) | collective-permute-done | bytes 1572896 | tf_op jit(solution)/shard_map/ppermute | solution.py:218
  45.4 3.1 %collective-permute-done.13.a3 = bf16[4,768,256]{2,1,0:T(8,128)(2,1)} collective-permute-done((bf16[4,768,256]{2,1,0:T(8,128)(2,1)}, bf16[4,768,256]{2,1,0:T(8,128)(2,1)}, u32[]{:S(2)}, u32[]{:S(2)}) %collective-permute-start.13) | collective-permute-done | bytes 1572896 | tf_op jit(solution)/shard_map/ppermute | solution.py:281
  48.6 1.2 copy-done.4
  49.8 25.1 %attn.5 = (bf16[16,192,1024]{2,1,0:T(8,128)(2,1)}, bf16[16,192,1024]{2,1,0:T(8,128)(2,1)}, bf16[4,256,384]{2,1,0:T(8,128)(2,1)S(1)}, bf16[4,256,384]{2,1,0:T(8,128)(2,1)S(1)}) custom-call(s32[9]{0:T(128)S(1)} %stack.52.idx_ref, s32[16]{0:T(128)S(1)} %copy-done.8, s32[1]{0:T(128)} %constant.15.clone.1.row_ref, bf16[4,768,256]{2,1,0:T(8,128)(2,1)S(1)} %copy-done.1, ...), custom_call_target="tpu_custom_call" | custom-call | flops 24000000000 | bytes 16000000 | tf_op jit(solution)/shard_map/attn/pallas_call | solution.py:321
  75.0 7.0 %collective-permute-done.7.a2 = bf16[4,768,256]{2,1,0:T(8,128)(2,1)} collective-permute-done((bf16[4,768,256]{2,1,0:T(8,128)(2,1)}, bf16[4,768,256]{2,1,0:T(8,128)(2,1)}, u32[]{:S(2)}, u32[]{:S(2)}) %collective-permute-start.7) | collective-permute-done | bytes 1572896 | tf_op jit(solution)/shard_map/ppermute | solution.py:218
  82.0 0.3 collective-permute-start.5
  82.5 3.1 %collective-permute-done.14.a3 = bf16[4,768,256]{2,1,0:T(8,128)(2,1)S(1)} collective-permute-done((bf16[4,768,256]{2,1,0:T(8,128)(2,1)}, bf16[4,768,256]{2,1,0:T(8,128)(2,1)S(1)}, u32[]{:S(2)}, u32[]{:S(2)}) %collective-permute-start.14) | collective-permute-done | bytes 1572896 | tf_op jit(solution)/shard_map/ppermute | solution.py:281
  85.6 25.4 %attn.6 = (bf16[16,192,1024]{2,1,0:T(8,128)(2,1)}, bf16[16,192,1024]{2,1,0:T(8,128)(2,1)}, bf16[4,256,384]{2,1,0:T(8,128)(2,1)S(1)}, bf16[4,256,384]{2,1,0:T(8,128)(2,1)S(1)}) custom-call(s32[9]{0:T(128)S(1)} %stack.52.idx_ref, s32[16]{0:T(128)S(1)} %copy-done.8, s32[1]{0:T(128)} %constant.14.clone.1.row_ref, ...), custom_call_target="tpu_custom_call", output_to_operand_aliasing={{0}: (11, {}), {1}: (12, {})} | custom-call | flops 24000000000 | bytes 16000000 | tf_op jit(solution)/shard_map/attn/pallas_call | solution.py:321
  111.2 0.4 collective-permute-start.16
  111.6 2.0 %collective-permute-start.3 = (bf16[3,768,256]{2,1,0:T(8,128)(2,1)S(1)}, bf16[3,768,256]{2,1,0:T(8,128)(2,1)S(1)}, u32[]{:S(2)}, u32[]{:S(2)}) collective-permute-start(bf16[3,768,256]{2,1,0:T(8,128)(2,1)S(1)} %copy-done.2), channel_id=1, source_target_pairs={{0,2},{1,3},{2,0},{3,1},{4,6},{5,7},{6,4},{7,5}} | collective-permute-start | bytes 3538952 | tf_op jit(solution)/shard_map/ppermute | solution.py:218
  113.6 1.5 collective-permute-done.16.other_ref
  115.0 3.8 %dense.5.rest_0_ = bf16[16,256,768]{2,1,0:T(8,128)(2,1)} custom-call(s32[9]{0:T(128)S(1)} %stack.52.idx_ref, s32[1]{0:T(128)} %constant.15.clone.1.row_ref, bf16[4,256,384]{2,1,0:T(8,128)(2,1)S(1)} %get-tuple-element.45.own_ref, bf16[4,256,384]{2,1,0:T(8,128)(2,1)S(1)} %collective-permute-done.16.other_ref, bf16[4,768,256]{2,1,0:T(8,128)(2,1)S(1)} %copy-done.1, ...), custom_call_target="tpu_custom_call" | custom-call | flops 4000000000 | bytes 8000000 | tf_op jit(solution)/shard_map/dense/pallas_call | solution.py:257
  118.8 18.4 %attn.7 = (bf16[16,192,1024]{2,1,0:T(8,128)(2,1)}, bf16[16,192,1024]{2,1,0:T(8,128)(2,1)}, bf16[3,256,384]{2,1,0:T(8,128)(2,1)S(1)}, bf16[3,256,384]{2,1,0:T(8,128)(2,1)S(1)}) custom-call(s32[9]{0:T(128)S(1)} %stack.52.idx_ref, s32[16]{0:T(128)S(1)} %copy-done.8, s32[1]{0:T(128)} %constant.13.clone.1.row_ref, ...), custom_call_target="tpu_custom_call", output_to_operand_aliasing={{0}: (11, {}), {1}: (12, {})} | custom-call | flops 17999998976 | bytes 12000000 | tf_op jit(solution)/shard_map/attn/pallas_call | solution.py:321
  137.2 2.6 %collective-permute-done.3.a2 = bf16[3,768,256]{2,1,0:T(8,128)(2,1)S(1)} collective-permute-done((bf16[3,768,256]{2,1,0:T(8,128)(2,1)S(1)}, bf16[3,768,256]{2,1,0:T(8,128)(2,1)S(1)}, u32[]{:S(2)}, u32[]{:S(2)}) %collective-permute-start.3) | collective-permute-done | bytes 1179680 | tf_op jit(solution)/shard_map/ppermute | solution.py:218
  139.8 0.5 collective-permute-start.18
  140.3 1.7 collective-permute-start.1
  142.1 1.7 collective-permute-done.18.other_ref
  143.8 5.2 %dense.6.rest_0_ = bf16[16,256,768]{2,1,0:T(8,128)(2,1)} custom-call(s32[9]{0:T(128)S(1)} %stack.52.idx_ref, s32[1]{0:T(128)} %constant.14.clone.1.row_ref, bf16[4,256,384]{2,1,0:T(8,128)(2,1)S(1)} %get-tuple-element.49.own_ref, bf16[4,256,384]{2,1,0:T(8,128)(2,1)S(1)} %collective-permute-done.18.other_ref, ...), custom_call_target="tpu_custom_call", output_to_operand_aliasing={{}: (10, {})} | custom-call | flops 4000000000 | bytes 8000000 | tf_op jit(solution)/shard_map/dense/pallas_call | solution.py:257
  149.0 18.6 %attn.8 = (bf16[16,192,1024]{2,1,0:T(8,128)(2,1)}, bf16[16,192,1024]{2,1,0:T(8,128)(2,1)}, bf16[3,256,384]{2,1,0:T(8,128)(2,1)S(1)}, bf16[3,256,384]{2,1,0:T(8,128)(2,1)S(1)}) custom-call(s32[9]{0:T(128)S(1)} %stack.52.idx_ref, s32[16]{0:T(128)S(1)} %copy-done.8, s32[1]{0:T(128)} %constant.21.clone.1.row_ref, ...), custom_call_target="tpu_custom_call", output_to_operand_aliasing={{0}: (11, {}), {1}: (12, {})} | custom-call | flops 17999998976 | bytes 12000000 | tf_op jit(solution)/shard_map/attn/pallas_call | solution.py:321
  167.8 0.4 collective-permute-start.22
  168.3 1.6 collective-permute-done.19.a3
  169.9 12.7 %attn.9 = (bf16[16,192,1024]{2,1,0:T(8,128)(2,1)}, bf16[16,192,1024]{2,1,0:T(8,128)(2,1)}, bf16[2,256,384]{2,1,0:T(8,128)(2,1)S(1)}, bf16[2,256,384]{2,1,0:T(8,128)(2,1)S(1)}) custom-call(s32[9]{0:T(128)S(1)} %stack.52.idx_ref, s32[16]{0:T(128)S(1)} %copy-done.8, s32[1]{0:T(128)} %constant.20.clone.1.row_ref, ...), custom_call_target="tpu_custom_call", output_to_operand_aliasing={{0}: (11, {}), {1}: (12, {})} | custom-call | flops 12000000000 | bytes 8000000 | tf_op jit(solution)/shard_map/attn/pallas_call | solution.py:321
  182.7 3.2 %dense.7.rest_0_ = bf16[16,256,768]{2,1,0:T(8,128)(2,1)} custom-call(s32[9]{0:T(128)S(1)} %stack.52.idx_ref, s32[1]{0:T(128)} %constant.13.clone.1.row_ref, bf16[3,256,384]{2,1,0:T(8,128)(2,1)S(1)} %get-tuple-element.53.own_ref, bf16[3,256,384]{2,1,0:T(8,128)(2,1)S(1)} %collective-permute-done.22.other_ref, ...), custom_call_target="tpu_custom_call", output_to_operand_aliasing={{}: (10, {})} | custom-call | flops 3000000000 | bytes 6000000 | tf_op jit(solution)/shard_map/dense/pallas_call | solution.py:257
  185.9 3.2 %dense.8.rest_0_ = bf16[16,256,768]{2,1,0:T(8,128)(2,1)} custom-call(s32[9]{0:T(128)S(1)} %stack.52.idx_ref, s32[1]{0:T(128)} %constant.21.clone.1.row_ref, bf16[3,256,384]{2,1,0:T(8,128)(2,1)S(1)} %get-tuple-element.58.own_ref, bf16[3,256,384]{2,1,0:T(8,128)(2,1)S(1)} %collective-permute-done.21.other_ref, ...), custom_call_target="tpu_custom_call", output_to_operand_aliasing={{}: (10, {})} | custom-call | flops 3000000000 | bytes 6000000 | tf_op jit(solution)/shard_map/dense/pallas_call | solution.py:257
  189.1 2.5 %dense.9 = bf16[16,256,768]{2,1,0:T(8,128)(2,1)} custom-call(s32[9]{0:T(128)S(1)} %stack.52.idx_ref, s32[1]{0:T(128)} %constant.20.clone.1.row_ref, bf16[2,256,384]{2,1,0:T(8,128)(2,1)S(1)} %get-tuple-element.63.own_ref, bf16[2,256,384]{2,1,0:T(8,128)(2,1)S(1)} %collective-permute-done.20.other_ref, ...), custom_call_target="tpu_custom_call", output_to_operand_aliasing={{}: (10, {})} | custom-call | flops 2000000000 | bytes 4000000 | tf_op jit(solution)/shard_map/dense/pallas_call | solution.py:257
  (77 shorter events, 2.5 us)
Async XLA Ops:
  0.6 7.7 %copy-start.9 = (f32[16,256]{1,0:T(8,128)S(1)}, f32[16,256]{1,0:T(8,128)}, u32[]{:S(2)}) copy-start(f32[16,256]{1,0:T(8,128)} %constant.47) | copy-start | bytes 49156
  4.4 15.4 %collective-permute-start.11 = (s32[1,16]{1,0:T(1,128)S(1)}, s32[1,16]{1,0:T(1,128)S(1)}, u32[]{:S(2)}, u32[]{:S(2)}) collective-permute-start(s32[1,16]{1,0:T(1,128)S(1)} %bitcast.54), channel_id=1, source_target_pairs={{0,2},{1,3},{2,0},{3,1},{4,6},{5,7},{6,4},{7,5}} | collective-permute-start | bytes 200 | tf_op jit(solution)/shard_map/ppermute | solution.py:225
  7.7 12.2 %collective-permute-start.10 = (s32[1,16]{1,0:T(1,128)S(1)}, s32[1,16]{1,0:T(1,128)S(1)}, u32[]{:S(2)}, u32[]{:S(2)}) collective-permute-start(s32[1,16]{1,0:T(1,128)S(1)} %bitcast.55), channel_id=1, source_target_pairs={{0,1},{1,0},{2,3},{3,2},{4,5},{5,4},{6,7},{7,6}} | collective-permute-start | bytes 200 | tf_op jit(solution)/shard_map/ppermute | solution.py:226
  7.7 37.1 %collective-permute-start.9 = (bf16[4,768,256]{2,1,0:T(8,128)(2,1)}, bf16[4,768,256]{2,1,0:T(8,128)(2,1)}, u32[]{:S(2)}, u32[]{:S(2)}) collective-permute-start(bf16[4,768,256]{2,1,0:T(8,128)(2,1)} %norm.3.a0.a_ref), channel_id=1, source_target_pairs={{0,2},{1,3},{2,0},{3,1},{4,6},{5,7},{6,4},{7,5}} | collective-permute-start | bytes 4718600 | tf_op jit(solution)/shard_map/ppermute | solution.py:218
  7.8 37.7 %collective-permute-start.8 = (bf16[4,768,256]{2,1,0:T(8,128)(2,1)}, bf16[4,768,256]{2,1,0:T(8,128)(2,1)}, u32[]{:S(2)}, u32[]{:S(2)}) collective-permute-start(bf16[4,768,256]{2,1,0:T(8,128)(2,1)} %norm.3.a0.a_ref), channel_id=1, source_target_pairs={{0,1},{1,0},{2,3},{3,2},{4,5},{5,4},{6,7},{7,6}} | collective-permute-start | bytes 4718600 | tf_op jit(solution)/shard_map/ppermute | solution.py:221
  8.5 12.5 %copy-start.15 = (f32[16]{0:T(128)S(1)}, f32[16]{0:T(128)}, u32[]{:S(2)}) copy-start(f32[16]{0:T(128)} %constant.42.clone) | copy-start | bytes 196
  19.8 1.2 collective-permute-start.12
  25.0 23.6 %copy-start.1 = (bf16[4,768,256]{2,1,0:T(8,128)(2,1)S(1)}, bf16[4,768,256]{2,1,0:T(8,128)(2,1)}, u32[]{:S(2)}) copy-start(bf16[4,768,256]{2,1,0:T(8,128)(2,1)} %norm.3.a0.a_ref) | copy-start | bytes 4718596
  44.8 3.8 %collective-permute-start.13 = (bf16[4,768,256]{2,1,0:T(8,128)(2,1)}, bf16[4,768,256]{2,1,0:T(8,128)(2,1)}, u32[]{:S(2)}, u32[]{:S(2)}) collective-permute-start(bf16[4,768,256]{2,1,0:T(8,128)(2,1)} %collective-permute-done.9.a2), channel_id=1, source_target_pairs={{0,1},{1,0},{2,3},{3,2},{4,5},{5,4},{6,7},{7,6}} | collective-permute-start | bytes 4718600 | tf_op jit(solution)/shard_map/ppermute | solution.py:281
  44.8 37.1 %collective-permute-start.7 = (bf16[4,768,256]{2,1,0:T(8,128)(2,1)}, bf16[4,768,256]{2,1,0:T(8,128)(2,1)}, u32[]{:S(2)}, u32[]{:S(2)}) collective-permute-start(bf16[4,768,256]{2,1,0:T(8,128)(2,1)} %get-tuple-element.39.a0.a_ref), channel_id=1, source_target_pairs={{0,2},{1,3},{2,0},{3,1},{4,6},{5,7},{6,4},{7,5}} | collective-permute-start | bytes 4718600 | tf_op jit(solution)/shard_map/ppermute | solution.py:218
  45.1 37.4 %collective-permute-start.6 = (bf16[4,768,256]{2,1,0:T(8,128)(2,1)}, bf16[4,768,256]{2,1,0:T(8,128)(2,1)}, u32[]{:S(2)}, u32[]{:S(2)}) collective-permute-start(bf16[4,768,256]{2,1,0:T(8,128)(2,1)} %get-tuple-element.39.a0.a_ref), channel_id=1, source_target_pairs={{0,1},{1,0},{2,3},{3,2},{4,5},{5,4},{6,7},{7,6}} | collective-permute-start | bytes 4718600 | tf_op jit(solution)/shard_map/ppermute | solution.py:221
  45.4 36.5 %copy-start.3 = (bf16[3,768,256]{2,1,0:T(8,128)(2,1)S(1)}, bf16[3,768,256]{2,1,0:T(8,128)(2,1)}, u32[]{:S(2)}) copy-start(bf16[3,768,256]{2,1,0:T(8,128)(2,1)} %get-tuple-element.38.a0.a_ref) | copy-start | bytes 3538948
  49.8 35.7 %copy-start.5 = (f32[2176,128]{1,0:T(8,128)S(1)}, f32[2176,128]{1,0:T(8,128)}, u32[]{:S(2)}) copy-start(f32[2176,128]{1,0:T(8,128)} %broadcast.33.col_ref.bias_ref) | copy-start | bytes 3342340
  82.0 3.6 %collective-permute-start.14 = (bf16[4,768,256]{2,1,0:T(8,128)(2,1)}, bf16[4,768,256]{2,1,0:T(8,128)(2,1)S(1)}, u32[]{:S(2)}, u32[]{:S(2)}) collective-permute-start(bf16[4,768,256]{2,1,0:T(8,128)(2,1)} %collective-permute-done.7.a2), channel_id=1, source_target_pairs={{0,1},{1,0},{2,3},{3,2},{4,5},{5,4},{6,7},{7,6}} | collective-permute-start | bytes 4718600 | tf_op jit(solution)/shard_map/ppermute | solution.py:281
  82.0 29.1 %collective-permute-start.5 = (bf16[3,768,256]{2,1,0:T(8,128)(2,1)S(1)}, bf16[3,768,256]{2,1,0:T(8,128)(2,1)S(1)}, u32[]{:S(2)}, u32[]{:S(2)}) collective-permute-start(bf16[3,768,256]{2,1,0:T(8,128)(2,1)S(1)} %copy-done.3), channel_id=1, source_target_pairs={{0,2},{1,3},{2,0},{3,1},{4,6},{5,7},{6,4},{7,5}} | collective-permute-start | bytes 3538952 | tf_op jit(solution)/shard_map/ppermute | solution.py:218
  82.3 36.6 %collective-permute-start.4 = (bf16[3,768,256]{2,1,0:T(8,128)(2,1)S(1)}, bf16[3,768,256]{2,1,0:T(8,128)(2,1)S(1)}, u32[]{:S(2)}, u32[]{:S(2)}) collective-permute-start(bf16[3,768,256]{2,1,0:T(8,128)(2,1)S(1)} %copy-done.3), channel_id=1, source_target_pairs={{0,1},{1,0},{2,3},{3,2},{4,5},{5,4},{6,7},{7,6}} | collective-permute-start | bytes 3538952 | tf_op jit(solution)/shard_map/ppermute | solution.py:221
  85.6 26.0 %copy-start.2 = (bf16[3,768,256]{2,1,0:T(8,128)(2,1)S(1)}, bf16[3,768,256]{2,1,0:T(8,128)(2,1)}, u32[]{:S(2)}) copy-start(bf16[3,768,256]{2,1,0:T(8,128)(2,1)} %get-tuple-element.37.a0.a_ref) | copy-start | bytes 3538948
  85.6 29.4 %copy-start = (bf16[768,768]{1,0:T(8,128)(2,1)S(1)}, bf16[768,768]{1,0:T(8,128)(2,1)}, u32[]{:S(2)}) copy-start(bf16[768,768]{1,0:T(8,128)(2,1)} %param.22) | copy-start | bytes 3538948
  85.6 29.4 %copy-start.7 = (bf16[768]{0:T(1024)(128)(2,1)S(1)}, bf16[768]{0:T(1024)(128)(2,1)}, u32[]{:S(2)}) copy-start(bf16[768]{0:T(1024)(128)(2,1)} %b_ref.13) | copy-start | bytes 4612
  111.0 7.8 %collective-permute-start.15 = (bf16[3,768,256]{2,1,0:T(8,128)(2,1)S(1)}, bf16[3,768,256]{2,1,0:T(8,128)(2,1)S(1)}, u32[]{:S(2)}, u32[]{:S(2)}) collective-permute-start(bf16[3,768,256]{2,1,0:T(8,128)(2,1)S(1)} %collective-permute-done.5.a2), channel_id=1, source_target_pairs={{0,1},{1,0},{2,3},{3,2},{4,5},{5,4},{6,7},{7,6}} | collective-permute-start | bytes 3538952 | tf_op jit(solution)/shard_map/ppermute | solution.py:281
  111.2 3.8 %collective-permute-start.16 = (bf16[4,256,384]{2,1,0:T(8,128)(2,1)S(1)}, bf16[4,256,384]{2,1,0:T(8,128)(2,1)S(1)}, u32[]{:S(2)}, u32[]{:S(2)}) collective-permute-start(bf16[4,256,384]{2,1,0:T(8,128)(2,1)S(1)} %get-tuple-element.54), channel_id=1, source_target_pairs={{0,1},{1,0},{2,3},{3,2},{4,5},{5,4},{6,7},{7,6}} | collective-permute-start | bytes 2359304 | tf_op jit(solution)/shard_map/ppermute | solution.py:322
  111.6 28.2 %collective-permute-start.3 = (bf16[3,768,256]{2,1,0:T(8,128)(2,1)S(1)}, bf16[3,768,256]{2,1,0:T(8,128)(2,1)S(1)}, u32[]{:S(2)}, u32[]{:S(2)}) collective-permute-start(bf16[3,768,256]{2,1,0:T(8,128)(2,1)S(1)} %copy-done.2), channel_id=1, source_target_pairs={{0,2},{1,3},{2,0},{3,1},{4,6},{5,7},{6,4},{7,5}} | collective-permute-start | bytes 3538952 | tf_op jit(solution)/shard_map/ppermute | solution.py:218
  113.6 35.4 %collective-permute-start.2 = (bf16[3,768,256]{2,1,0:T(8,128)(2,1)S(1)}, bf16[3,768,256]{2,1,0:T(8,128)(2,1)S(1)}, u32[]{:S(2)}, u32[]{:S(2)}) collective-permute-start(bf16[3,768,256]{2,1,0:T(8,128)(2,1)S(1)} %copy-done.2), channel_id=1, source_target_pairs={{0,1},{1,0},{2,3},{3,2},{4,5},{5,4},{6,7},{7,6}} | collective-permute-start | bytes 3538952 | tf_op jit(solution)/shard_map/ppermute | solution.py:221
  118.8 21.5 %copy-start.6 = (bf16[2,768,256]{2,1,0:T(8,128)(2,1)S(1)}, bf16[2,768,256]{2,1,0:T(8,128)(2,1)}, u32[]{:S(2)}) copy-start(bf16[2,768,256]{2,1,0:T(8,128)(2,1)} %get-tuple-element.36.a0.a_ref) | copy-start | bytes 2359300
  139.8 9.2 %collective-permute-start.17 = (bf16[3,768,256]{2,1,0:T(8,128)(2,1)S(1)}, bf16[3,768,256]{2,1,0:T(8,128)(2,1)S(1)}, u32[]{:S(2)}, u32[]{:S(2)}) collective-permute-start(bf16[3,768,256]{2,1,0:T(8,128)(2,1)S(1)} %collective-permute-done.3.a2), channel_id=1, source_target_pairs={{0,1},{1,0},{2,3},{3,2},{4,5},{5,4},{6,7},{7,6}} | collective-permute-start | bytes 3538952 | tf_op jit(solution)/shard_map/ppermute | solution.py:281
  139.8 4.0 %collective-permute-start.18 = (bf16[4,256,384]{2,1,0:T(8,128)(2,1)S(1)}, bf16[4,256,384]{2,1,0:T(8,128)(2,1)S(1)}, u32[]{:S(2)}, u32[]{:S(2)}) collective-permute-start(bf16[4,256,384]{2,1,0:T(8,128)(2,1)S(1)} %get-tuple-element.59), channel_id=1, source_target_pairs={{0,1},{1,0},{2,3},{3,2},{4,5},{5,4},{6,7},{7,6}} | collective-permute-start | bytes 2359304 | tf_op jit(solution)/shard_map/ppermute | solution.py:322
  140.3 27.3 %collective-permute-start.1 = (bf16[2,768,256]{2,1,0:T(8,128)(2,1)S(1)}, bf16[2,768,256]{2,1,0:T(8,128)(2,1)S(1)}, u32[]{:S(2)}, u32[]{:S(2)}) collective-permute-start(bf16[2,768,256]{2,1,0:T(8,128)(2,1)S(1)} %copy-done.6), channel_id=1, source_target_pairs={{0,2},{1,3},{2,0},{3,1},{4,6},{5,7},{6,4},{7,5}} | collective-permute-start | bytes 2359304 | tf_op jit(solution)/shard_map/ppermute | solution.py:218
  142.1 26.2 %collective-permute-start = (bf16[2,768,256]{2,1,0:T(8,128)(2,1)S(1)}, bf16[2,768,256]{2,1,0:T(8,128)(2,1)S(1)}, u32[]{:S(2)}, u32[]{:S(2)}) collective-permute-start(bf16[2,768,256]{2,1,0:T(8,128)(2,1)S(1)} %copy-done.6), channel_id=1, source_target_pairs={{0,1},{1,0},{2,3},{3,2},{4,5},{5,4},{6,7},{7,6}} | collective-permute-start | bytes 2359304 | tf_op jit(solution)/shard_map/ppermute | solution.py:221
  167.6 2.3 %collective-permute-start.19 = (bf16[2,768,256]{2,1,0:T(8,128)(2,1)S(1)}, bf16[2,768,256]{2,1,0:T(8,128)(2,1)S(1)}, u32[]{:S(2)}, u32[]{:S(2)}) collective-permute-start(bf16[2,768,256]{2,1,0:T(8,128)(2,1)S(1)} %collective-permute-done.1.a2), channel_id=1, source_target_pairs={{0,1},{1,0},{2,3},{3,2},{4,5},{5,4},{6,7},{7,6}} | collective-permute-start | bytes 2359304 | tf_op jit(solution)/shard_map/ppermute | solution.py:281
  167.8 15.0 %collective-permute-start.22 = (bf16[3,256,384]{2,1,0:T(8,128)(2,1)S(1)}, bf16[3,256,384]{2,1,0:T(8,128)(2,1)S(1)}, u32[]{:S(2)}, u32[]{:S(2)}) collective-permute-start(bf16[3,256,384]{2,1,0:T(8,128)(2,1)S(1)} %get-tuple-element.66), channel_id=1, source_target_pairs={{0,1},{1,0},{2,3},{3,2},{4,5},{5,4},{6,7},{7,6}} | collective-permute-start | bytes 1769480 | tf_op jit(solution)/shard_map/ppermute | solution.py:322
  168.1 17.8 %collective-permute-start.21 = (bf16[3,256,384]{2,1,0:T(8,128)(2,1)S(1)}, bf16[3,256,384]{2,1,0:T(8,128)(2,1)S(1)}, u32[]{:S(2)}, u32[]{:S(2)}) collective-permute-start(bf16[3,256,384]{2,1,0:T(8,128)(2,1)S(1)} %get-tuple-element.65), channel_id=1, source_target_pairs={{0,1},{1,0},{2,3},{3,2},{4,5},{5,4},{6,7},{7,6}} | collective-permute-start | bytes 1769480 | tf_op jit(solution)/shard_map/ppermute | solution.py:322
  182.6 6.6 %collective-permute-start.20 = (bf16[2,256,384]{2,1,0:T(8,128)(2,1)S(1)}, bf16[2,256,384]{2,1,0:T(8,128)(2,1)S(1)}, u32[]{:S(2)}, u32[]{:S(2)}) collective-permute-start(bf16[2,256,384]{2,1,0:T(8,128)(2,1)S(1)} %get-tuple-element.64), channel_id=1, source_target_pairs={{0,1},{1,0},{2,3},{3,2},{4,5},{5,4},{6,7},{7,6}} | collective-permute-start | bytes 1179656 | tf_op jit(solution)/shard_map/ppermute | solution.py:322
  (7 other events, 43.0 us)
